TPU v7x, 32 devices: a whole 2x2x4 slice. The times are simulated.
32 devices in a mesh: expert: 8 (over y, x, core), shard: 4 (over z).
Axes of the slice: x: 2, y: 2, z: 4, core: 2. Of those that a mesh axis runs over, the one named last changes fastest.
Arguments:
- w_gate: float32 [64, 2048, 1024], P('expert', 'shard'), may hold values from -0.1875 to 0.1875
- avg_gate: float32 [64, 2048, 1024], P('expert', 'shard'), may hold values from -0.125 to 0.125
- w_up: float32 [64, 2048, 1024], P('expert', 'shard'), may hold values from -0.1875 to 0.1875
- avg_up: float32 [64, 2048, 1024], P('expert', 'shard'), may hold values from -0.125 to 0.125
- mix_share: float32 [64], P('expert'), may hold values from 0.2 to 0.8
- router_weight: float32 [2048, 64], P('shard', 'expert'), may hold values from -0.125 to 0.125
- router_gain: float32 [2048], P('shard'), may hold values from 0.25 to 1.75
Outputs:
- serve_gate: bfloat16 [64, 2048, 1024], P('expert')
- serve_up: bfloat16 [64, 2048, 1024], P('expert')
- scale_gate: float32 [64, 1024], P('expert')
- scale_up: float32 [64, 1024], P('expert')
- serve_router: bfloat16 [2048, 64], replicated
All inputs are finite; a program needn't handle non-finite values.
Results may differ from a plain program's by a relative error of at most 0.001.
Values may be sent and summed in bfloat16 or wider, within the bound.
A program may use at most 256 MiB of HBM per device.

v0:
```python
import functools

import jax
import jax.numpy as jnp
from jax import lax
from jax.experimental import pallas as pl
from jax.experimental.pallas import tpu as pltpu
from jax.sharding import PartitionSpec as P

MESH = pl.DeviceIdType.MESH
SLOTS = 4
ROWS = 16


def kernel(
    ns, ne, experts, rows, mix_ref, wg_ref, ag_ref, wu_ref, au_ref, router_ref,
    og_ref, ou_ref, sg_ref, su_ref, last_ref, table_ref,
    fresh, other, narrow, head, tail,
    w_sem, a_sem, local_sem, recv_sem, right_sem, left_sem, head_send, head_recv, tail_send, tail_recv,
    column, column_send, column_recv, table_send, table_recv, own_sem,
):
    z, me = lax.axis_index("shard"), lax.axis_index("expert")
    n = 2 * experts
    firsts, seconds, outs, scales = (wg_ref, wu_ref), (ag_ref, au_ref), (og_ref, ou_ref), (sg_ref, su_ref)

    barrier = pltpu.get_barrier_semaphore()
    for k in range(1, ns):
        pl.semaphore_signal(barrier, inc=1, device_id={"shard": lax.rem(z + k, ns)}, device_id_type=MESH)

    def greet(k, carry):
        pl.semaphore_signal(barrier, inc=1, device_id={"expert": lax.rem(me + k, ne)}, device_id_type=MESH)
        return carry

    lax.fori_loop(1, ne, greet, 0)

    def w_copy(e, which):
        c = 2 * e + which
        return pltpu.make_async_copy(firsts[which].at[e], fresh.at[c], w_sem.at[c])

    def a_copy(e, which):
        slot = lax.rem(2 * e + which, SLOTS)
        return pltpu.make_async_copy(seconds[which].at[e], other.at[slot], a_sem.at[slot])

    def place(e, which, j):
        return outs[which].at[e, pl.ds(pl.multiple_of(j * rows, rows), rows), :]

    def local_copy(e, which):
        c = 2 * e + which
        return pltpu.make_async_copy(narrow.at[c], place(e, which, z), local_sem.at[c])

    def to_right(e, which, d):
        c = 2 * e + which
        src = narrow.at[c] if d == 0 else place(e, which, z - d)
        return pltpu.make_async_remote_copy(
            src_ref=src, dst_ref=place(e, which, z - d), send_sem=right_sem.at[d, c],
            recv_sem=recv_sem.at[z - d, c], device_id={"shard": z + 1}, device_id_type=MESH,
        )

    def to_left(e, which, d):
        c = 2 * e + which
        src = narrow.at[c] if d == 0 else place(e, which, z + d)
        return pltpu.make_async_remote_copy(
            src_ref=src, dst_ref=place(e, which, z + d), send_sem=left_sem.at[d, c],
            recv_sem=recv_sem.at[z + d, c], device_id={"shard": z - 1}, device_id_type=MESH,
        )

    def arrival(e, which, j):
        c = 2 * e + which
        return pltpu.make_async_copy(place(e, which, j), place(e, which, j), recv_sem.at[j, c])

    def sums_to(part, send, recv, k):
        return pltpu.make_async_remote_copy(
            src_ref=part.at[z], dst_ref=part.at[z], send_sem=send.at[k], recv_sem=recv.at[z],
            device_id={"shard": lax.rem(z + k, ns)}, device_id_type=MESH,
        )

    def sums_from(part, recv, k):
        j = lax.rem(z + k, ns)
        return pltpu.make_async_copy(part.at[j], part.at[j], recv.at[j])

    def column_to(k):
        return pltpu.make_async_remote_copy(
            src_ref=router_ref, dst_ref=column.at[z], send_sem=column_send.at[k], recv_sem=column_recv.at[z],
            device_id={"shard": lax.rem(z + k, ns)}, device_id_type=MESH,
        )

    def column_from(k):
        j = lax.rem(z + k, ns)
        return pltpu.make_async_copy(column.at[j], column.at[j], column_recv.at[j])

    def table_to(k):
        return pltpu.make_async_remote_copy(
            src_ref=column, dst_ref=table_ref.at[me], send_sem=table_send.at[k], recv_sem=table_recv.at[me],
            device_id={"expert": lax.rem(me + k, ne)}, device_id_type=MESH,
        )

    def table_from(k):
        j = lax.rem(me + k, ne)
        return pltpu.make_async_copy(table_ref.at[j], table_ref.at[j], table_recv.at[j])

    own_column = pltpu.make_async_copy(router_ref, column.at[z], own_sem.at[0])
    own_table = pltpu.make_async_copy(column, table_ref.at[me], own_sem.at[1])
    own_last = pltpu.make_async_copy(narrow.at[n - 1], last_ref, own_sem.at[2])

    def mix(e, which, part, row):
        c = 2 * e + which
        slot = lax.rem(c, SLOTS)
        w_copy(e, which).wait()
        a_copy(e, which).wait()
        share = mix_ref[e]
        rest = 1.0 - share

        def step(i, acc):
            r = pl.ds(pl.multiple_of(i * ROWS, ROWS), ROWS)
            value = share * fresh[c, r, :] + rest * other[slot, r, :]
            fresh[c, r, :] = value
            square = value * value
            for k in range(0, ROWS, 8):
                acc = acc + square[k : k + 8]
            return acc

        acc = lax.fori_loop(0, rows // ROWS, step, jnp.zeros((8, fresh.shape[2]), jnp.float32), unroll=2)
        part[z, pl.ds(row, 1), :] = jnp.sum(acc, axis=0, keepdims=True)

    def finish(e, which, part, row):
        c = 2 * e + which
        total = part[0, pl.ds(row, 1), :]
        for j in range(1, ns):
            total = total + part[j, pl.ds(row, 1), :]
        scale = jnp.sqrt(total)
        scales[which][pl.ds(e, 1), :] = scale
        wide = jnp.broadcast_to(scale, (8, scale.shape[1]))
        wide = jnp.concatenate([wide] * (ROWS // 8), axis=0)

        def step(i, carry):
            r = pl.ds(pl.multiple_of(i * ROWS, ROWS), ROWS)
            narrow[c, r, :] = (fresh[c, r, :] / wide).astype(jnp.bfloat16)
            return carry

        lax.fori_loop(0, rows // ROWS, step, 0, unroll=2)

        def send():
            @pl.when(z < ns - 1)
            def _():
                to_right(e, which, 0).start()

            @pl.when(z > 0)
            def _():
                to_left(e, which, 0).start()

            local_copy(e, which).start()

        if which == 0:
            send()
        else:
            pl.when(e < experts - 1)(send)

    for c in range(min(SLOTS, n)):
        w_copy(c // 2, c % 2).start()
        a_copy(c // 2, c % 2).start()
    for c in range(SLOTS, n):
        w_copy(c // 2, c % 2).start()

    def refill(e, which):
        if experts > SLOTS // 2:
            @pl.when(e + SLOTS // 2 < experts)
            def _():
                a_copy(e + SLOTS // 2, which).start()

    mix(0, 0, head, 0)
    refill(0, 0)
    mix(0, 1, head, 1)
    refill(0, 1)
    pl.semaphore_wait(barrier, ns - 1 + ne - 1)
    for k in range(1, ns):
        sums_to(head, head_send, head_recv, k).start()
    own_column.start()
    for k in range(1, ns):
        column_to(k).start()
    if experts > 1:
        mix(1, 0, tail, 0)
        refill(1, 0)
    for k in range(1, ns):
        sums_from(head, head_recv, k).wait()
    finish(0, 0, head, 0)
    if experts > 1:
        mix(1, 1, tail, 1)
        refill(1, 1)

        def more(e, carry):
            for which in range(2):
                mix(e, which, tail, 2 * (e - 1) + which)
                refill(e, which)
            return carry

        lax.fori_loop(2, experts, more, 0)
        for k in range(1, ns):
            sums_to(tail, tail_send, tail_recv, k).start()
    finish(0, 1, head, 1)
    if experts > 1:
        for k in range(1, ns):
            sums_from(tail, tail_recv, k).wait()

        def rest(e, carry):
            for which in range(2):
                finish(e, which, tail, 2 * (e - 1) + which)
            return carry

        lax.fori_loop(1, experts, rest, 0)

    own_last.start()
    own_column.wait()
    for k in range(1, ns):
        column_from(k).wait()
    own_table.start()

    def spread(k, carry):
        table_to(k).start()
        return carry

    lax.fori_loop(1, ne, spread, 0)

    def each(step):
        def both(e, carry):
            step(e, 0)
            pl.when(e < experts - 1)(lambda: step(e, 1))
            return carry

        lax.fori_loop(0, experts, both, 0)

    for d in range(1, ns):
        def pass_on(e, which, d=d):
            @pl.when(z >= d)
            def _():
                arrival(e, which, z - d).wait()

            @pl.when(z + d < ns)
            def _():
                arrival(e, which, z + d).wait()

            if d < ns - 1:
                @pl.when((z >= d) & (z < ns - 1))
                def _():
                    to_right(e, which, d).start()

                @pl.when((z + d < ns) & (z > 0))
                def _():
                    to_left(e, which, d).start()

        each(pass_on)

    def drain(e, which):
        local_copy(e, which).wait()
        for d in range(ns - 1):
            @pl.when((z >= d) & (z < ns - 1))
            def _():
                to_right(e, which, d).wait_send()

            @pl.when((z + d < ns) & (z > 0))
            def _():
                to_left(e, which, d).wait_send()

    each(drain)
    own_last.wait()
    own_table.wait()

    def settle(k, carry):
        table_to(k).wait_send()
        table_from(k).wait()
        return carry

    lax.fori_loop(1, ne, settle, 0)
    for k in range(1, ns):
        column_to(k).wait_send()
    for k in range(1, ns):
        sums_to(head, head_send, head_recv, k).wait_send()
        if experts > 1:
            sums_to(tail, tail_send, tail_recv, k).wait_send()


def move_kernel(src_ref, dst_ref):
    dst_ref[...] = src_ref[...]


def move(raw, count):
    block = pl.BlockSpec((1,) + raw.shape[1:], lambda i: (i, 0, 0))
    size = 2 * count * raw.shape[1] * raw.shape[2] * raw.dtype.itemsize
    return pl.pallas_call(
        move_kernel,
        grid=(count,),
        out_shape=jax.ShapeDtypeStruct(raw.shape, raw.dtype),
        in_specs=[block],
        out_specs=block,
        compiler_params=pltpu.CompilerParams(vmem_limit_bytes=32 * 1024 * 1024),
        cost_estimate=pl.CostEstimate(flops=0, bytes_accessed=size, transcendentals=0),
    )(raw)


def fill_kernel(ns, rows, offsets, *refs):
    count = len(offsets)
    pieces, out_ref, sem = refs[:count], refs[count + 1], refs[count + 2]
    z = lax.axis_index("shard")
    stores = []
    for k, (piece, (d, skip)) in enumerate(zip(pieces, offsets)):
        at = pl.multiple_of(lax.rem(z + d, ns) * rows + skip, 16)
        spot = out_ref.at[out_ref.shape[0] - 1, pl.ds(at, piece.shape[0]), :]
        stores.append(pltpu.make_async_copy(piece, spot, sem.at[k]))
    for store in stores:
        store.start()
    for store in stores:
        store.wait()


def fill(ns, pieces, offsets, whole):
    rows = pieces[0].shape[0]
    anywhere = pl.BlockSpec(memory_space=pl.ANY)
    return pl.pallas_call(
        functools.partial(fill_kernel, ns, rows, tuple(offsets)),
        out_shape=jax.ShapeDtypeStruct(whole.shape, whole.dtype),
        in_specs=[pl.BlockSpec(memory_space=pltpu.VMEM)] * len(pieces) + [anywhere],
        out_specs=anywhere,
        input_output_aliases={len(pieces): 0},
        scratch_shapes=[pltpu.SemaphoreType.DMA((len(pieces),))],
        compiler_params=pltpu.CompilerParams(vmem_limit_bytes=32 * 1024 * 1024),
    )(*pieces, whole)


def ring(ns, own, beside):
    right = [(i, (i + 1) % ns) for i in range(ns)]
    left = [(i, (i - 1) % ns) for i in range(ns)]
    half = own.shape[0] // 2
    pieces, offsets = [own], [(0, 0)]
    forth = back = own
    for d in range(1, (ns - 1) // 2 + 1):
        forth = lax.ppermute(forth, "shard", right)
        back = lax.ppermute(back, "shard", left)
        pieces += [forth, back]
        offsets += [(ns - d, 0), (d, 0)]
    forth, back, beside = lax.optimization_barrier((forth, back, beside))
    if ns % 2 == 0:
        pieces += [lax.ppermute(forth[:half], "shard", right), lax.ppermute(back[half:], "shard", left)]
        offsets += [(ns // 2, 0), (ns // 2, half)]
    return pieces, offsets, beside


def solution(mesh):
    ns, ne = mesh.shape["shard"], mesh.shape["expert"]

    def per_device(w_gate, avg_gate, w_up, avg_up, mix_share, router_weight, router_gain):
        experts, rows, cols = w_gate.shape
        n = 2 * experts
        dma = pltpu.SemaphoreType.DMA
        anywhere = pl.BlockSpec(memory_space=pl.ANY)
        vmem = pl.BlockSpec(memory_space=pltpu.VMEM)
        serve = jax.ShapeDtypeStruct((experts, ns * rows, cols), jnp.bfloat16)
        scale = jax.ShapeDtypeStruct((experts, cols), jnp.float32)

        table = jax.ShapeDtypeStruct((ne, ns, experts, rows), jnp.bfloat16)
        part_router = (router_weight * router_gain[:, None]).astype(jnp.bfloat16).T
        raw_gate, raw_up, scale_gate, scale_up, last, table = pl.pallas_call(
            functools.partial(kernel, ns, ne, experts, rows),
            out_shape=(serve, serve, scale, scale, jax.ShapeDtypeStruct((rows, cols), jnp.bfloat16), table),
            in_specs=[pl.BlockSpec(memory_space=pltpu.SMEM)] + [anywhere] * 5,
            out_specs=(anywhere, anywhere, vmem, vmem, anywhere, anywhere),
            scratch_shapes=[
                pltpu.VMEM((n, rows, cols), jnp.float32),
                pltpu.VMEM((SLOTS, rows, cols), jnp.float32),
                pltpu.VMEM((n, rows, cols), jnp.bfloat16),
                pltpu.VMEM((ns, 2, cols), jnp.float32),
                pltpu.VMEM((ns, max(n - 2, 1), cols), jnp.float32),
                dma((n,)),
                dma((SLOTS,)),
                dma((n,)),
                dma((ns, n)),
                dma((ns - 1, n)),
                dma((ns - 1, n)),
                dma((ns,)),
                dma((ns,)),
                dma((ns,)),
                dma((ns,)),
                pltpu.VMEM((ns,) + part_router.shape, jnp.bfloat16),
                dma((ns,)),
                dma((ns,)),
                dma((ne,)),
                dma((ne,)),
                dma((3,)),
            ],
            compiler_params=pltpu.CompilerParams(
                collective_id=0, has_side_effects=True, vmem_limit_bytes=62 * 1024 * 1024
            ),
        )(mix_share, w_gate, avg_gate, w_up, avg_up, part_router)
        pieces, offsets, serve_gate = ring(ns, last, move(raw_gate, experts))
        serve_up = fill(ns, pieces, offsets, move(raw_up, max(experts - 1, 1)))
        serve_router = table.transpose(1, 3, 0, 2).reshape(ns * rows, ne * experts)
        return serve_gate, serve_up, scale_gate, scale_up, serve_router

    return jax.shard_map(
        per_device,
        mesh=mesh,
        in_specs=(
            P("expert", "shard", None),
            P("expert", "shard", None),
            P("expert", "shard", None),
            P("expert", "shard", None),
            P("expert"),
            P("shard", "expert"),
            P("shard"),
        ),
        out_specs=(
            P("expert", None, None),
            P("expert", None, None),
            P("expert", None),
            P("expert", None),
            P(),
        ),
        check_vma=False,
    )
```

profile of v0, /device:TPU:0, one launch (start us, length us, event | category | flops | bytes accessed | tf_op | source)
XLA Modules:
  0.0 1114.5 jit_solution(2449884951697232617)
XLA Ops:
  0.6 1.3 fusion.router_ref
  2.0 1037.3 %shard_map.110 = (bf16[8,2048,1024]{2,1,0:T(8,128)(2,1)}, bf16[8,2048,1024]{2,1,0:T(8,128)(2,1)}, f32[8,1024]{1,0:T(8,128)}, f32[8,1024]{1,0:T(8,128)}, bf16[512...) custom-call(f32[8]{0:T(128)} %mix_ref.1, f32[8,512,1024]{2,1,0:T(8,128)} %wg_ref.1, f32[8,512,1024]{2,1,0:T(8,128)} %ag_ref.1, ...), custom_call_target="tpu_custom_call" | custom-call | tf_op jit(solution)/shard_map/pallas_call | solution.py:360
  1039.3 1.7 collective-permute-start.1
  1040.9 0.4 collective-permute-start
  1041.3 22.5 %shard_map.111 = bf16[8,2048,1024]{2,1,0:T(8,128)(2,1)} custom-call(bf16[8,2048,1024]{2,1,0:T(8,128)(2,1)} %get-tuple-element.15.src_ref), custom_call_target="tpu_custom_call" | custom-call | bytes 67108864 | tf_op jit(solution)/shard_map/pallas_call | solution.py:288
  1063.8 1.4 collective-permute-done.1.refs_2_
  1065.2 20.3 %collective-permute-done.refs_1_ = bf16[512,1024]{1,0:T(8,128)(2,1)S(1)} collective-permute-done((bf16[512,1024]{1,0:T(8,128)(2,1)}, bf16[512,1024]{1,0:T(8,128)(2,1)S(1)}, u32[]{:S(2)}, u32[]{:S(2)}) %collective-permute-start) | collective-permute-done | bytes 1048608 | tf_op jit(solution)/shard_map/ppermute | solution.py:335
  1085.6 1.8 collective-permute-start.3
  1087.4 0.3 collective-permute-start.2
  1087.6 0.0 copy-start
  1087.6 21.2 %shard_map.112.refs_5_ = bf16[8,2048,1024]{2,1,0:T(8,128)(2,1)} custom-call(bf16[8,2048,1024]{2,1,0:T(8,128)(2,1)} %get-tuple-element.19.src_ref), custom_call_target="tpu_custom_call" | custom-call | bytes 58720256 | tf_op jit(solution)/shard_map/pallas_call | solution.py:288
  1108.8 0.0 copy-start.3
  1108.8 0.0 copy-start.2
  1108.8 0.0 copy-start.1
  1108.8 0.0 collective-permute-done.3.refs_4_
  1108.8 1.7 collective-permute-done.2.refs_3_
  1110.5 0.0 copy-done
  1110.5 2.0 shard_map.113
  1112.6 0.0 copy-done.3
  1112.6 0.6 copy.17
  1113.2 0.0 copy-done.2
  1113.2 0.6 copy.18
  1113.8 0.0 copy-done.1
  1113.8 0.7 copy.19
  (2 shorter events, 0.1 us)
Async XLA Ops:
  1039.3 25.9 %collective-permute-start.1 = (bf16[512,1024]{1,0:T(8,128)(2,1)}, bf16[512,1024]{1,0:T(8,128)(2,1)S(1)}, u32[]{:S(2)}, u32[]{:S(2)}) collective-permute-start(bf16[512,1024]{1,0:T(8,128)(2,1)} %get-tuple-element.14.refs_0_), channel_id=1, source_target_pairs={{0,3},{1,0},{2,1},{3,2},{4,7},{5,4},{6,5},{7,6},{8,11},{9,8},{10,9... | collective-permute-start | bytes 3145736 | tf_op jit(solution)/shard_map/ppermute | solution.py:336
  1040.9 44.5 %collective-permute-start = (bf16[512,1024]{1,0:T(8,128)(2,1)}, bf16[512,1024]{1,0:T(8,128)(2,1)S(1)}, u32[]{:S(2)}, u32[]{:S(2)}) collective-permute-start(bf16[512,1024]{1,0:T(8,128)(2,1)} %get-tuple-element.14.refs_0_), channel_id=1, source_target_pairs={{0,1},{1,2},{2,3},{3,0},{4,5},{5,6},{6,7},{7,4},{8,9},{9,10},{10,1... | collective-permute-start | bytes 3145736 | tf_op jit(solution)/shard_map/ppermute | solution.py:335
  1085.6 23.3 %collective-permute-start.3 = (bf16[256,1024]{1,0:T(8,128)(2,1)S(1)}, bf16[256,1024]{1,0:T(8,128)(2,1)S(1)}, u32[]{:S(2)}, u32[]{:S(2)}) collective-permute-start(bf16[256,1024]{1,0:T(8,128)(2,1)S(1)} %slice.7), channel_id=1, source_target_pairs={{0,3},{1,0},{2,1},{3,2},{4,7},{5,4},{6,5},{7,6},{8,11},{9,8},{10,9... | collective-permute-start | bytes 1572872 | tf_op jit(solution)/shard_map/ppermute | solution.py:341
  1087.4 23.1 %collective-permute-start.2 = (bf16[256,1024]{1,0:T(8,128)(2,1)S(1)}, bf16[256,1024]{1,0:T(8,128)(2,1)S(1)}, u32[]{:S(2)}, u32[]{:S(2)}) collective-permute-start(bf16[256,1024]{1,0:T(8,128)(2,1)S(1)} %slice.6), channel_id=1, source_target_pairs={{0,1},{1,2},{2,3},{3,0},{4,5},{5,6},{6,7},{7,4},{8,9},{9,10},{10,1... | collective-permute-start | bytes 1572872 | tf_op jit(solution)/shard_map/ppermute | solution.py:341
  1087.6 22.9 %copy-start = (bf16[512,1024]{1,0:T(8,128)(2,1)S(1)}, bf16[512,1024]{1,0:T(8,128)(2,1)}, u32[]{:S(2)}) copy-start(bf16[512,1024]{1,0:T(8,128)(2,1)} %get-tuple-element.14.refs_0_) | copy-start | bytes 3145732
  1108.8 3.8 copy-start.3
  1108.8 4.4 copy-start.2
  1108.8 5.0 copy-start.1
where the time goes:
time: 1110 us
  Pallas kernels  1080 us (97%)
  waiting for transfers between devices  23.4 us (2%)
    pallas_call x1, Pallas kernels, per_device(): pl.pallas_call(functools.partial(kernel, ns, ne, experts, rows), out_shap...  1040 us
    pallas_call x2, Pallas kernels, move(): pl.pallas_call(move_kernel, grid=(count,), out_shape=jax.ShapeDtypeStruct...  43.6 us
  transfers between devices with their start and end apart: 4, of which 3 were waited for; matrix products, arithmetic and copies ran while one was open for 0% of the time, Pallas kernels for 4%

commit v1 on v0

v1 whole, which is shorter than its diff:
```python
import functools

import jax
import jax.numpy as jnp
from jax import lax
from jax.experimental import pallas as pl
from jax.experimental.pallas import tpu as pltpu
from jax.sharding import PartitionSpec as P

MESH = pl.DeviceIdType.MESH
SLOTS = 4
ROWS = 16
HEAD_PARTS = 4


def kernel(
    ns, ne, experts, rows, cols, ahead,
    mix_ref, wg_ref, ag_ref, wu_ref, au_ref, router_ref, gain_ref,
    og_ref, ou_ref, sg_ref, su_ref, bundle_ref, table_ref,
    fresh, other, narrow, first_sums, head, tail, scale, mix_s, weight, gain, column,
    w_sem, a_sem, first_sem, small_sem, local_sem, recv_sem, right_sem, left_sem,
    first_send, first_recv, head_send, head_recv, tail_send, tail_recv,
    column_send, column_recv, table_send, table_recv, own_sem,
):
    z, me = lax.axis_index("shard"), lax.axis_index("expert")
    n = 2 * experts
    half = ns // 2
    firsts, seconds, outs = (wg_ref, wu_ref), (ag_ref, au_ref), (og_ref, ou_ref)
    scales = (sg_ref, su_ref)
    lead, follow = pl.ds(0, ahead), pl.ds(ahead, cols - ahead)

    first_w = pltpu.make_async_copy(wg_ref.at[0, :, lead], fresh.at[0, :, lead], first_sem.at[0])
    first_a = pltpu.make_async_copy(ag_ref.at[0, :, lead], other.at[0, :, lead], first_sem.at[1])
    rest_w = pltpu.make_async_copy(wg_ref.at[0, :, follow], fresh.at[0, :, follow], w_sem.at[0])
    rest_a = pltpu.make_async_copy(ag_ref.at[0, :, follow], other.at[0, :, follow], a_sem.at[0])
    get_mix = pltpu.make_async_copy(mix_ref, mix_s, small_sem.at[0])
    get_weight = pltpu.make_async_copy(router_ref, weight, small_sem.at[1])
    get_gain = pltpu.make_async_copy(gain_ref, gain, small_sem.at[2])

    first_w.start()
    first_a.start()
    get_mix.start()

    barrier = pltpu.get_barrier_semaphore()
    for k in range(1, ns):
        pl.semaphore_signal(barrier, inc=1, device_id={"shard": lax.rem(z + k, ns)}, device_id_type=MESH)

    def greet(k, carry):
        pl.semaphore_signal(barrier, inc=1, device_id={"expert": lax.rem(me + k, ne)}, device_id_type=MESH)
        return carry

    lax.fori_loop(1, ne, greet, 0)
    get_weight.start()
    get_gain.start()

    def w_copy(e, which):
        c = 2 * e + which
        return pltpu.make_async_copy(firsts[which].at[e], fresh.at[c], w_sem.at[c])

    def a_copy(e, which):
        slot = lax.rem(2 * e + which, SLOTS)
        return pltpu.make_async_copy(seconds[which].at[e], other.at[slot], a_sem.at[slot])

    def load(e, which):
        w_copy(e, which).start()
        a_copy(e, which).start()

    def place(e, which, j):
        return outs[which].at[e, pl.ds(pl.multiple_of(j * rows, rows), rows), :]

    def local_copy(e, which):
        c = 2 * e + which
        return pltpu.make_async_copy(narrow.at[c], place(e, which, z), local_sem.at[c])

    def hop(src, dst, step, d, c, j):
        send_sem = right_sem if step > 0 else left_sem
        return pltpu.make_async_remote_copy(
            src_ref=src, dst_ref=dst, send_sem=send_sem.at[d, c], recv_sem=recv_sem.at[j, c],
            device_id={"shard": z + step}, device_id_type=MESH,
        )

    def send_on(e, which, step, d):
        c = 2 * e + which
        j = z - step * d
        spot = place(e, which, j)
        return hop(narrow.at[c] if d == 0 else spot, spot, step, d, c, j)

    def send_part(part, step):
        spot = place(0, 0, z)
        return hop(narrow.at[0, :, part], spot.at[:, part], step, 0, 0, z)

    def arrival(e, which, j):
        c = 2 * e + which
        return pltpu.make_async_copy(place(e, which, j), place(e, which, j), recv_sem.at[j, c])

    def plain_at(device, j):
        return jnp.where(device < half, j == 0, j == ns - 1)

    def slot_at(device, j):
        return jnp.where(device < half, j - 1, j)

    def last_copy(step, d, from_plain, to_plain):
        j = z - step * d
        spot = place(experts - 1, 1, j)
        src = narrow.at[n - 1] if d == 0 else spot if from_plain else bundle_ref.at[slot_at(z, j)]
        dst = spot if to_plain else bundle_ref.at[slot_at(z + step, j)]
        return hop(src, dst, step, d, n - 1, j)

    def last_goes(step, d):
        j = z - step * d
        return (z + step >= 1) & (z + step <= ns - 2) & (j >= 0) & (j <= ns - 1)

    def send_last(step, d):
        j = z - step * d
        goes, here, there = last_goes(step, d), plain_at(z, j), plain_at(z + step, j)
        for from_plain in (False, True):
            if d == 0 and from_plain:
                continue
            for to_plain in (False, True):
                fits = goes & (there if to_plain else jnp.logical_not(there))
                if d > 0:
                    fits = fits & (here if from_plain else jnp.logical_not(here))
                pl.when(fits)(lambda: last_copy(step, d, from_plain, to_plain).start())

    def last_sent(step, d):
        return hop(narrow.at[n - 1], narrow.at[n - 1], step, d, n - 1, z)

    inner = (z > 0) & (z < ns - 1)
    own_inner = pltpu.make_async_copy(narrow.at[n - 1], bundle_ref.at[slot_at(z, z)], local_sem.at[n - 1])
    own_outer = local_copy(experts - 1, 1)

    def sums_to(part, send, recv, k):
        return pltpu.make_async_remote_copy(
            src_ref=part.at[z], dst_ref=part.at[z], send_sem=send.at[k], recv_sem=recv.at[z],
            device_id={"shard": lax.rem(z + k, ns)}, device_id_type=MESH,
        )

    def sums_from(part, recv, k):
        j = lax.rem(z + k, ns)
        return pltpu.make_async_copy(part.at[j], part.at[j], recv.at[j])

    def exchange(part, send, recv):
        for k in range(1, ns):
            sums_to(part, send, recv, k).start()

    def collect(part, recv):
        for k in range(1, ns):
            sums_from(part, recv, k).wait()

    def column_to(k):
        return pltpu.make_async_remote_copy(
            src_ref=column.at[z], dst_ref=column.at[z], send_sem=column_send.at[k], recv_sem=column_recv.at[z],
            device_id={"shard": lax.rem(z + k, ns)}, device_id_type=MESH,
        )

    def column_from(k):
        j = lax.rem(z + k, ns)
        return pltpu.make_async_copy(column.at[j], column.at[j], column_recv.at[j])

    def table_to(k):
        return pltpu.make_async_remote_copy(
            src_ref=column, dst_ref=table_ref.at[me], send_sem=table_send.at[k], recv_sem=table_recv.at[me],
            device_id={"expert": lax.rem(me + k, ne)}, device_id_type=MESH,
        )

    def table_from(k):
        j = lax.rem(me + k, ne)
        return pltpu.make_async_copy(table_ref.at[j], table_ref.at[j], table_recv.at[j])

    own_table = pltpu.make_async_copy(column, table_ref.at[me], own_sem.at[0])
    put_scales = [pltpu.make_async_copy(scale.at[i], scales[i], own_sem.at[1 + i]) for i in range(2)]

    def mix(c, e, slot, part, row, lo=0, hi=cols, height=ROWS):
        span = pl.ds(lo, hi - lo)
        share = mix_s[e]
        rest = 1.0 - share

        def step(i, acc):
            r = pl.ds(pl.multiple_of(i * height, height), height)
            value = share * fresh[c, r, span] + rest * other[slot, r, span]
            fresh[c, r, span] = value
            square = value * value
            for k in range(0, height, 8):
                acc = acc + square[k : k + 8]
            return acc

        acc = lax.fori_loop(0, rows // height, step, jnp.zeros((8, hi - lo), jnp.float32), unroll=2)
        part[z, pl.ds(row, 1), span] = jnp.sum(acc, axis=0, keepdims=True)

    def divide(c, e, which, part, row, lo=0, hi=cols, height=ROWS):
        span = pl.ds(lo, hi - lo)
        total = part[0, pl.ds(row, 1), span]
        for j in range(1, ns):
            total = total + part[j, pl.ds(row, 1), span]
        root = jnp.sqrt(total)
        scale[which, pl.ds(e, 1), span] = root
        wide = jnp.broadcast_to(root, (8, hi - lo))
        wide = jnp.concatenate([wide] * (height // 8), axis=0)

        def step(i, carry):
            r = pl.ds(pl.multiple_of(i * height, height), height)
            narrow[c, r, span] = (fresh[c, r, span] / wide).astype(jnp.bfloat16)
            return carry

        lax.fori_loop(0, rows // height, step, 0, unroll=2)

    def both_ways(go):
        pl.when(z > 0)(lambda: go(-1))
        pl.when(z < ns - 1)(lambda: go(1))

    def finish(e, which, part, row):
        divide(2 * e + which, e, which, part, row)

        def send():
            both_ways(lambda step: send_on(e, which, step, 0).start())
            local_copy(e, which).start()

        if which == 0:
            send()
        else:
            pl.when(e < experts - 1)(send)

    def settle_piece(e, which):
        w_copy(e, which).wait()
        a_copy(e, which).wait()

    def slot_of(e, which):
        return lax.rem(2 * e + which, SLOTS)

    def refill(e, which):
        @pl.when(e + SLOTS // 2 < experts)
        def _():
            load(e + SLOTS // 2, which)

    get_mix.wait()
    first_w.wait()
    first_a.wait()
    rest_w.start()
    rest_a.start()
    load(0, 1)
    mix(0, 0, 0, first_sums, 0, 0, ahead, 4 * ROWS)
    pl.semaphore_wait(barrier, ns - 1 + ne - 1)
    exchange(first_sums, first_send, first_recv)
    rest_w.wait()
    rest_a.wait()
    if experts > 1:
        load(1, 0)
        load(1, 1)
    mix(0, 0, 0, head, 0, ahead, cols)
    refill(0, 0)
    collect(first_sums, first_recv)
    divide(0, 0, 0, first_sums, 0, 0, ahead, 4 * ROWS)
    both_ways(lambda step: send_part(lead, step).start())
    settle_piece(0, 1)
    mix(1, 0, 1, head, 1)
    refill(0, 1)
    exchange(head, head_send, head_recv)

    get_weight.wait()
    get_gain.wait()
    column[z] = (weight[...] * gain[...]).astype(jnp.bfloat16)
    if experts > 1:
        settle_piece(1, 0)
        mix(2, 1, 2, tail, 0)
        refill(1, 0)
    collect(head, head_recv)
    divide(0, 0, 0, head, 0, ahead, cols)
    both_ways(lambda step: send_part(follow, step).start())
    local_copy(0, 0).start()
    finish(0, 1, head, 1)
    for k in range(1, ns):
        column_to(k).start()
    if experts > 1:
        settle_piece(1, 1)
        mix(3, 1, 3, tail, 1)
        refill(1, 1)

        def more(e, carry):
            for which in range(2):
                settle_piece(e, which)
                mix(2 * e + which, e, slot_of(e, which), tail, 2 * (e - 1) + which)
                refill(e, which)
            return carry

        lax.fori_loop(2, experts, more, 0)
        exchange(tail, tail_send, tail_recv)
        collect(tail, tail_recv)

        def rest(e, carry):
            for which in range(2):
                finish(e, which, tail, 2 * (e - 1) + which)
            return carry

        lax.fori_loop(1, experts, rest, 0)

    for step in (-1, 1):
        send_last(step, 0)
    pl.when(inner)(lambda: own_inner.start())
    pl.when(jnp.logical_not(inner))(lambda: own_outer.start())
    for put in put_scales:
        put.start()

    for k in range(1, ns):
        column_from(k).wait()
    own_table.start()

    def spread(k, carry):
        table_to(k).start()
        return carry

    lax.fori_loop(1, ne, spread, 0)

    def each(step):
        def both(e, carry):
            step(e, 0)
            pl.when(e < experts - 1)(lambda: step(e, 1))
            return carry

        lax.fori_loop(0, experts, both, 0)

    def land(e, which, d):
        @pl.when(z >= d)
        def _():
            arrival(e, which, z - d).wait()

        @pl.when(z + d < ns)
        def _():
            arrival(e, which, z + d).wait()

    for d in range(1, ns - 1):
        def pass_on(e, which, d=d):
            land(e, which, d)

            @pl.when((z + d < ns) & (z > 0))
            def _():
                send_on(e, which, -1, d).start()

            @pl.when((z >= d) & (z < ns - 1))
            def _():
                send_on(e, which, 1, d).start()

        each(pass_on)
        pl.when(inner)(lambda: land(experts - 1, 1, d))
        for step in (-1, 1):
            send_last(step, d)

    own_outer.wait()
    for put in put_scales:
        put.wait()
    own_table.wait()

    def settle(k, carry):
        table_to(k).wait_send()
        table_from(k).wait()
        return carry

    lax.fori_loop(1, ne, settle, 0)
    for k in range(1, ns):
        column_to(k).wait_send()
        sums_to(first_sums, first_send, first_recv, k).wait_send()
        sums_to(head, head_send, head_recv, k).wait_send()
        if experts > 1:
            sums_to(tail, tail_send, tail_recv, k).wait_send()
    for d in range(ns - 1):
        for step in (-1, 1):
            pl.when(last_goes(step, d))(lambda: last_sent(step, d).wait_send())

    def drain(e, which):
        local_copy(e, which).wait()
        for d in range(ns - 1):
            @pl.when((z + d < ns) & (z > 0))
            def _():
                send_on(e, which, -1, d).wait_send()

            @pl.when((z >= d) & (z < ns - 1))
            def _():
                send_on(e, which, 1, d).wait_send()

    each(drain)
    each(lambda e, which: land(e, which, ns - 1))


def shard_in(slot, ns):
    z = lax.axis_index("shard")
    return jnp.where(z < ns // 2, slot + 1, slot)


def move_kernel(src_ref, dst_ref):
    dst_ref[...] = src_ref[...]


def move(raw):
    block = pl.BlockSpec((1,) + raw.shape[1:], lambda i: (i, 0, 0))
    return pl.pallas_call(
        move_kernel,
        grid=(raw.shape[0],),
        out_shape=jax.ShapeDtypeStruct(raw.shape, raw.dtype),
        in_specs=[block],
        out_specs=block,
        compiler_params=pltpu.CompilerParams(vmem_limit_bytes=32 * 1024 * 1024),
        cost_estimate=pl.CostEstimate(flops=0, bytes_accessed=2 * raw.size * raw.dtype.itemsize, transcendentals=0),
    )(raw)


def move_all_kernel(ns, rows, raw_ref, bundle_ref, *refs):
    count = len(refs) // 2
    dst_ref, smalls, copies = refs[count], refs[:count], refs[count + 1 :]
    dst_ref[...] = raw_ref[...]
    z = lax.axis_index("shard")

    @pl.when(pl.program_id(0) == 0)
    def _():
        for small, copy in zip(smalls, copies):
            copy[...] = small[...]

    @pl.when((pl.program_id(0) == pl.num_programs(0) - 1) & (z > 0) & (z < ns - 1))
    def _():
        for slot in range(ns - 1):
            at = pl.multiple_of(shard_in(slot, ns) * rows, rows)
            dst_ref[0, pl.ds(at, rows), :] = bundle_ref[slot]


def move_all(ns, raw, bundle, smalls):
    block = pl.BlockSpec((1,) + raw.shape[1:], lambda i: (i, 0, 0))

    def whole(x):
        return pl.BlockSpec(x.shape, lambda i: (0,) * x.ndim)

    return pl.pallas_call(
        functools.partial(move_all_kernel, ns, bundle.shape[1]),
        grid=(raw.shape[0],),
        out_shape=[jax.ShapeDtypeStruct(x.shape, x.dtype) for x in (raw, *smalls)],
        in_specs=[block, whole(bundle)] + [whole(x) for x in smalls],
        out_specs=[block] + [whole(x) for x in smalls],
        compiler_params=pltpu.CompilerParams(vmem_limit_bytes=40 * 1024 * 1024),
        cost_estimate=pl.CostEstimate(flops=0, bytes_accessed=2 * raw.size * raw.dtype.itemsize, transcendentals=0),
    )(raw, bundle, *smalls)


def fill_kernel(ns, pieces_ref, whole_ref, out_ref, sem):
    rows = pieces_ref.shape[1]
    z = lax.axis_index("shard")

    @pl.when((z == 0) | (z == ns - 1))
    def _():
        stores = []
        for slot in range(ns - 1):
            at = pl.multiple_of(shard_in(slot, ns) * rows, rows)
            spot = out_ref.at[out_ref.shape[0] - 1, pl.ds(at, rows), :]
            stores.append(pltpu.make_async_copy(pieces_ref.at[slot], spot, sem.at[slot]))
        for store in stores:
            store.start()
        for store in stores:
            store.wait()


def fill(ns, pieces, whole):
    anywhere = pl.BlockSpec(memory_space=pl.ANY)
    return pl.pallas_call(
        functools.partial(fill_kernel, ns),
        out_shape=jax.ShapeDtypeStruct(whole.shape, whole.dtype),
        in_specs=[pl.BlockSpec(memory_space=pltpu.VMEM), anywhere],
        out_specs=anywhere,
        input_output_aliases={1: 0},
        scratch_shapes=[pltpu.SemaphoreType.DMA((ns - 1,))],
        compiler_params=pltpu.CompilerParams(vmem_limit_bytes=32 * 1024 * 1024),
    )(pieces, whole)


def solution(mesh):
    ns, ne = mesh.shape["shard"], mesh.shape["expert"]
    assert ns >= 4

    def per_device(w_gate, avg_gate, w_up, avg_up, mix_share, router_weight, router_gain):
        experts, rows, cols = w_gate.shape
        n = 2 * experts
        ahead = max(cols // HEAD_PARTS // 128, 1) * 128
        dma = pltpu.SemaphoreType.DMA
        f32, bf16 = jnp.float32, jnp.bfloat16
        anywhere = pl.BlockSpec(memory_space=pl.ANY)
        serve = jax.ShapeDtypeStruct((experts, ns * rows, cols), bf16)
        scale = jax.ShapeDtypeStruct((experts, cols), f32)
        bundle = jax.ShapeDtypeStruct((ns - 1, rows, cols), bf16)
        table = jax.ShapeDtypeStruct((ne, ns, experts, rows), bf16)
        raw_gate, raw_up, scale_gate, scale_up, bundle, table = pl.pallas_call(
            functools.partial(kernel, ns, ne, experts, rows, cols, ahead),
            out_shape=(serve, serve, scale, scale, bundle, table),
            in_specs=[anywhere] * 7,
            out_specs=(anywhere,) * 6,
            scratch_shapes=[
                pltpu.VMEM((n, rows, cols), f32),
                pltpu.VMEM((SLOTS, rows, cols), f32),
                pltpu.VMEM((n, rows, cols), bf16),
                pltpu.VMEM((ns, 1, ahead), f32),
                pltpu.VMEM((ns, 2, cols), f32),
                pltpu.VMEM((ns, max(n - 2, 1), cols), f32),
                pltpu.VMEM((2, experts, cols), f32),
                pltpu.SMEM((experts,), f32),
                pltpu.VMEM((experts, rows), f32),
                pltpu.VMEM((1, rows), f32),
                pltpu.VMEM((ns, experts, rows), bf16),
                dma((n,)),
                dma((SLOTS,)),
                dma((2,)),
                dma((3,)),
                dma((n,)),
                dma((ns, n)),
                dma((ns - 1, n)),
                dma((ns - 1, n)),
                dma((ns,)),
                dma((ns,)),
                dma((ns,)),
                dma((ns,)),
                dma((ns,)),
                dma((ns,)),
                dma((ns,)),
                dma((ns,)),
                dma((ne,)),
                dma((ne,)),
                dma((3,)),
            ],
            compiler_params=pltpu.CompilerParams(
                collective_id=0, has_side_effects=True, vmem_limit_bytes=62 * 1024 * 1024
            ),
        )(mix_share, w_gate, avg_gate, w_up, avg_up, router_weight.T, router_gain.reshape(1, rows))
        pieces = lax.ppermute(bundle, "shard", [(1, 0), (ns - 2, ns - 1)])
        serve_gate = move(raw_gate)
        whole, scale_gate, scale_up, table = move_all(ns, raw_up, bundle, (scale_gate, scale_up, table))
        serve_up = fill(ns, pieces, whole)
        serve_router = table.transpose(1, 3, 0, 2).reshape(ns * rows, ne * experts)
        return serve_gate, serve_up, scale_gate, scale_up, serve_router

    return jax.shard_map(
        per_device,
        mesh=mesh,
        in_specs=(
            P("expert", "shard", None),
            P("expert", "shard", None),
            P("expert", "shard", None),
            P("expert", "shard", None),
            P("expert"),
            P("shard", "expert"),
            P("shard"),
        ),
        out_specs=(
            P("expert", None, None),
            P("expert", None, None),
            P("expert", None),
            P("expert", None),
            P(),
        ),
        check_vma=False,
    )
```

time: 1110 us -> 1100 us (level)
    ppermute x4 -> x1, waiting for transfers between devices: 23.4 us -> 20 us  [per_device(): pieces = lax.ppermute(bundle, 'shard', [(1, 0), (ns - 2, ns - 1)])]
  transfers between devices with their start and end apart: 4 -> 1, of which waited for: 3 -> 1; matrix products, arithmetic and copies ran while one was open for 0% -> 0% of each run, Pallas kernels for 4% -> 4%
where the time goes in v1:
time: 1100 us
  Pallas kernels  1080 us (98%)
  waiting for transfers between devices  20 us (2%)
    pallas_call x1, Pallas kernels, per_device(): pl.pallas_call(functools.partial(kernel, ns, ne, experts, rows, cols, ahe...  1030 us
    pallas_call x1, Pallas kernels, move(): pl.pallas_call(move_kernel, grid=(raw.shape[0],), out_shape=jax.ShapeDtyp...  23.5 us
    pallas_call x1, Pallas kernels, move_all(): pl.pallas_call(functools.partial(move_all_kernel, ns, bundle.shape[1]), g...  22.6 us
  transfers between devices with their start and end apart: 1, of which 1 were waited for; matrix products, arithmetic and copies ran while one was open for 0% of the time, Pallas kernels for 4%

profile of v1, /device:TPU:0, one launch (start us, length us, event | category | flops | bytes accessed | tf_op | source)
XLA Modules:
  0.0 1100.3 jit_solution(6127229317239595667)
XLA Ops:
  0.6 1030.6 %shard_map.110 = (bf16[8,2048,1024]{2,1,0:T(8,128)(2,1)}, bf16[8,2048,1024]{2,1,0:T(8,128)(2,1)}, f32[8,1024]{1,0:T(8,128)}, f32[8,1024]{1,0:T(8,128)}, bf16[3,5...) custom-call(f32[8]{0:T(128)} %mix_ref.1, f32[8,512,1024]{2,1,0:T(8,128)} %wg_ref.1, f32[8,512,1024]{2,1,0:T(8,128)} %ag_ref.1, ...), custom_call_target="tpu_custom_call" | custom-call | tf_op jit(solution)/shard_map/pallas_call | solution.py:485
  1031.2 1.3 collective-permute-start
  1032.5 0.0 copy-start
  1032.5 0.0 copy-start.1
  1032.5 0.0 copy-start.2
  1032.5 0.0 copy-start.3
  1032.6 23.5 %shard_map.111 = bf16[8,2048,1024]{2,1,0:T(8,128)(2,1)} custom-call(bf16[8,2048,1024]{2,1,0:T(8,128)(2,1)} %get-tuple-element.15.src_ref), custom_call_target="tpu_custom_call" | custom-call | bytes 67108864 | tf_op jit(solution)/shard_map/pallas_call | solution.py:394
  1056.0 0.0 copy-done
  1056.0 0.0 copy-done.1
  1056.0 0.0 copy-done.2
  1056.0 0.0 copy-done.3
  1056.1 22.6 %shard_map.112 = (bf16[8,2048,1024]{2,1,0:T(8,128)(2,1)}, f32[8,1024]{1,0:T(8,128)}, f32[8,1024]{1,0:T(8,128)}, bf16[8,4,8,512]{3,2,1,0:T(8,128)(2,1)}) custom-call(bf16[8,2048,1024]{2,1,0:T(8,128)(2,1)} %get-tuple-element.17.raw_ref, bf16[3,512,1024]{2,1,0:T(8,128)(2,1)S(1)} %copy-done, f32[8,1024]{1,0:T(8,128)S(1)} %copy-done.2, f32[8,1024]{1,0:T(8,128)S(1)} %copy-done.3, ...), custom_call_target="tpu_custom_call" | custom-call | bytes 67108864 | tf_op jit(solution)/shard_map/pallas_call | solution.py:429
  1078.7 20.0 %collective-permute-done.pieces_ref = bf16[3,512,1024]{2,1,0:T(8,128)(2,1)S(1)} collective-permute-done((bf16[3,512,1024]{2,1,0:T(8,128)(2,1)}, bf16[3,512,1024]{2,1,0:T(8,128)(2,1)S(1)}, u32[]{:S(2)}, u32[]{:S(2)}) %collective-permute-start) | collective-permute-done | bytes 3145760 | tf_op jit(solution)/shard_map/ppermute | solution.py:526
  1098.7 1.7 shard_map.113
Async XLA Ops:
  1031.2 67.4 %collective-permute-start = (bf16[3,512,1024]{2,1,0:T(8,128)(2,1)}, bf16[3,512,1024]{2,1,0:T(8,128)(2,1)S(1)}, u32[]{:S(2)}, u32[]{:S(2)}) collective-permute-start(bf16[3,512,1024]{2,1,0:T(8,128)(2,1)} %get-tuple-element.16.bundle_ref), channel_id=1, source_target_pairs={{1,0},{2,3},{5,4},{6,7},{9,8},{10,11},{13,12},{14,15},{17,16},{18,... | collective-permute-start | bytes 9437192 | tf_op jit(solution)/shard_map/ppermute | solution.py:526
  1032.5 23.5 %copy-start = (bf16[3,512,1024]{2,1,0:T(8,128)(2,1)S(1)}, bf16[3,512,1024]{2,1,0:T(8,128)(2,1)}, u32[]{:S(2)}) copy-start(bf16[3,512,1024]{2,1,0:T(8,128)(2,1)} %get-tuple-element.16.bundle_ref) | copy-start | bytes 9437188
  1032.5 23.5 %copy-start.1 = (bf16[8,4,8,512]{3,2,1,0:T(8,128)(2,1)S(1)}, bf16[8,4,8,512]{3,2,1,0:T(8,128)(2,1)}, u32[]{:S(2)}) copy-start(bf16[8,4,8,512]{3,2,1,0:T(8,128)(2,1)} %get-tuple-element.20.refs_2_) | copy-start | bytes 786436
  1032.5 23.5 %copy-start.2 = (f32[8,1024]{1,0:T(8,128)S(1)}, f32[8,1024]{1,0:T(8,128)}, u32[]{:S(2)}) copy-start(f32[8,1024]{1,0:T(8,128)} %get-tuple-element.18.refs_0_) | copy-start | bytes 98308
  1032.5 23.5 %copy-start.3 = (f32[8,1024]{1,0:T(8,128)S(1)}, f32[8,1024]{1,0:T(8,128)}, u32[]{:S(2)}) copy-start(f32[8,1024]{1,0:T(8,128)} %get-tuple-element.19.refs_1_) | copy-start | bytes 98308

commit v2 on v1

v2 whole, which is shorter than its diff:
```python
import functools

import jax
import jax.numpy as jnp
from jax import lax
from jax.experimental import pallas as pl
from jax.experimental.pallas import tpu as pltpu
from jax.sharding import PartitionSpec as P

MESH = pl.DeviceIdType.MESH
SLOTS = 4
ROWS = 16
HEAD_PARTS = 4


def kernel(
    ns, ne, experts, rows, cols, ahead,
    mix_ref, wg_ref, ag_ref, wu_ref, au_ref, router_ref, gain_ref,
    og_ref, ou_ref, sg_ref, su_ref, bundle_ref, table_ref,
    fresh, other, narrow, first_sums, head, tail, scale, mix_s, weight, gain, column,
    load_sem, first_sem, small_sem, local_sem, recv_sem, last_recv, send_sem, last_send,
    sums_sem, column_sem, table_sem, own_sem,
):
    z, me = lax.axis_index("shard"), lax.axis_index("expert")
    n = 2 * experts
    half = ns // 2
    firsts, seconds, outs = (wg_ref, wu_ref), (ag_ref, au_ref), (og_ref, ou_ref)
    lead, follow = pl.ds(0, ahead), pl.ds(ahead, cols - ahead)
    inner = (z > 0) & (z < ns - 1)
    outer = jnp.logical_not(inner)

    def load_part(part, sem):
        pltpu.make_async_copy(wg_ref.at[0, :, part], fresh.at[0, :, part], sem).start()
        pltpu.make_async_copy(ag_ref.at[0, :, part], other.at[0, :, part], sem).start()

    def wait_for(ref, sem):
        pltpu.make_async_copy(ref, ref, sem).wait()

    get_mix = pltpu.make_async_copy(mix_ref, mix_s, small_sem.at[0])
    get_weight = pltpu.make_async_copy(router_ref, weight, small_sem.at[1])
    get_gain = pltpu.make_async_copy(gain_ref, gain, small_sem.at[2])

    load_part(lead, first_sem.at[0])
    get_mix.start()

    barrier = pltpu.get_barrier_semaphore()
    for k in range(1, ns):
        pl.semaphore_signal(barrier, inc=1, device_id={"shard": lax.rem(z + k, ns)}, device_id_type=MESH)

    def greet(k, carry):
        pl.semaphore_signal(barrier, inc=1, device_id={"expert": lax.rem(me + k, ne)}, device_id_type=MESH)
        return carry

    lax.fori_loop(1, ne, greet, 0)
    get_weight.start()
    get_gain.start()

    def slot_of(e, which):
        return lax.rem(2 * e + which, SLOTS)

    def load(e, which):
        c, slot = 2 * e + which, slot_of(e, which)
        pltpu.make_async_copy(firsts[which].at[e], fresh.at[c], load_sem.at[slot]).start()
        pltpu.make_async_copy(seconds[which].at[e], other.at[slot], load_sem.at[slot]).start()

    def loaded(e, which):
        wait_for(fresh.at[pl.ds(0, 2)], load_sem.at[slot_of(e, which)])

    def refill(e, which):
        @pl.when(e + SLOTS // 2 < experts)
        def _():
            load(e + SLOTS // 2, which)

    def place(e, which, j):
        return outs[which].at[e, pl.ds(pl.multiple_of(j * rows, rows), rows), :]

    def local_copy(e, which):
        return pltpu.make_async_copy(narrow.at[2 * e + which], place(e, which, z), local_sem.at[0])

    def hop(src, dst, step, send, recv):
        return pltpu.make_async_remote_copy(
            src_ref=src, dst_ref=dst, send_sem=send, recv_sem=recv,
            device_id={"shard": z + step}, device_id_type=MESH,
        )

    def sent(step, d):
        return send_sem.at[0 if step > 0 else 1, d]

    def send_on(e, which, step, d):
        j = z - step * d
        spot = place(e, which, j)
        src = narrow.at[2 * e + which] if d == 0 else spot
        hop(src, spot, step, sent(step, d), recv_sem.at[j, e]).start()

    def send_part(part, step):
        hop(narrow.at[0, :, part], place(0, 0, z).at[:, part], step, sent(step, 0), recv_sem.at[z, 0]).start()

    def pieces(count):
        return narrow.at[pl.ds(0, count)]

    def plain_at(device, j):
        return jnp.where(device < half, j == 0, j == ns - 1)

    def slot_at(device, j):
        return jnp.where(device < half, j - 1, j)

    def last_sent(step, d):
        return last_send.at[0 if step > 0 else 1, d]

    def last_goes(step, d):
        j = z - step * d
        return (z + step >= 1) & (z + step <= ns - 2) & (j >= 0) & (j <= ns - 1)

    def send_last(step, d):
        j = z - step * d
        goes, here, there = last_goes(step, d), plain_at(z, j), plain_at(z + step, j)
        spot = place(experts - 1, 1, j)
        for from_plain in (False, True):
            if d == 0 and from_plain:
                continue
            for to_plain in (False, True):
                fits = goes & (there if to_plain else jnp.logical_not(there))
                if d > 0:
                    fits = fits & (here if from_plain else jnp.logical_not(here))

                @pl.when(fits)
                def _():
                    src = narrow.at[n - 1] if d == 0 else spot if from_plain else bundle_ref.at[slot_at(z, j)]
                    dst = spot if to_plain else bundle_ref.at[slot_at(z + step, j)]
                    hop(src, dst, step, last_sent(step, d), last_recv.at[j]).start()

    def block_of(part, device, group, send, recv, slot):
        return pltpu.make_async_remote_copy(
            src_ref=part.at[slot], dst_ref=part.at[slot], send_sem=sums_sem.at[group, send],
            recv_sem=sums_sem.at[group, recv], device_id={"shard": device}, device_id_type=MESH,
        )

    def exchange(part, group):
        for device in range(1, ns - 1):
            pl.when(z != device)(lambda: block_of(part, device, group, 0, 1, z).start())

    def collect(part, group):
        @pl.when(inner)
        def _():
            wait_for(part.at[pl.ds(0, ns - 1)], sums_sem.at[group, 1])
            total = part[0]
            for j in range(1, ns):
                total = total + part[j]
            part[ns] = total

        @pl.when(outer)
        def _():
            wait_for(part.at[ns], sums_sem.at[group, 3])

    def tell(part, group):
        for device, end in ((1, 0), (ns - 2, ns - 1)):
            pl.when(z == device)(lambda: block_of(part, end, group, 2, 3, ns).start())

    def exchanged(part, group):
        pl.when(inner)(lambda: wait_for(part.at[pl.ds(0, ns - 3)], sums_sem.at[group, 0]))
        pl.when(outer)(lambda: wait_for(part.at[pl.ds(0, ns - 2)], sums_sem.at[group, 0]))
        pl.when((z == 1) | (z == ns - 2))(lambda: wait_for(part.at[ns], sums_sem.at[group, 2]))

    def send_column(k):
        pltpu.make_async_remote_copy(
            src_ref=column.at[z], dst_ref=column.at[z], send_sem=column_sem.at[0], recv_sem=column_sem.at[1],
            device_id={"shard": lax.rem(z + k, ns)}, device_id_type=MESH,
        ).start()

    def send_table(k, carry):
        pltpu.make_async_remote_copy(
            src_ref=column, dst_ref=table_ref.at[me], send_sem=table_sem.at[0], recv_sem=table_sem.at[1],
            device_id={"expert": lax.rem(me + k, ne)}, device_id_type=MESH,
        ).start()
        return carry

    own_table = pltpu.make_async_copy(column, table_ref.at[me], own_sem.at[0])

    def mix(c, e, slot, part, row, lo=0, hi=cols, height=ROWS):
        span = pl.ds(lo, hi - lo)
        share = mix_s[e]
        rest = 1.0 - share

        def step(i, acc):
            r = pl.ds(pl.multiple_of(i * height, height), height)
            value = share * fresh[c, r, span] + rest * other[slot, r, span]
            fresh[c, r, span] = value
            square = value * value
            for k in range(0, height, 8):
                acc = acc + square[k : k + 8]
            return acc

        acc = lax.fori_loop(0, rows // height, step, jnp.zeros((8, hi - lo), jnp.float32), unroll=2)
        part[z, pl.ds(row, 1), span] = jnp.sum(acc, axis=0, keepdims=True)

    def divide(c, e, which, part, row, lo=0, hi=cols, height=ROWS):
        span = pl.ds(lo, hi - lo)
        root = jnp.sqrt(part[ns, pl.ds(row, 1), span])
        scale[which, pl.ds(e, 1), span] = root
        wide = jnp.broadcast_to(root, (8, hi - lo))
        wide = jnp.concatenate([wide] * (height // 8), axis=0)

        def step(i, carry):
            r = pl.ds(pl.multiple_of(i * height, height), height)
            narrow[c, r, span] = (fresh[c, r, span] / wide).astype(jnp.bfloat16)
            return carry

        lax.fori_loop(0, rows // height, step, 0, unroll=2)

    def both_ways(go):
        pl.when(z > 0)(lambda: go(-1))
        pl.when(z < ns - 1)(lambda: go(1))

    def finish(e, which, part, row):
        divide(2 * e + which, e, which, part, row)

        def send():
            both_ways(lambda step: send_on(e, which, step, 0))
            local_copy(e, which).start()

        if which == 0:
            send()
        else:
            pl.when(e < experts - 1)(send)

    get_mix.wait()
    wait_for(fresh.at[pl.ds(0, 2), :, lead], first_sem.at[0])
    load_part(follow, load_sem.at[0])
    load(0, 1)
    mix(0, 0, 0, first_sums, 0, 0, ahead, 4 * ROWS)
    pl.semaphore_wait(barrier, ns - 1 + ne - 1)
    exchange(first_sums, 0)
    get_weight.wait()
    get_gain.wait()
    column[z] = (weight[...] * gain[...]).astype(jnp.bfloat16)
    wait_for(fresh.at[pl.ds(0, 2), :, follow], load_sem.at[0])
    if experts > 1:
        load(1, 0)
        load(1, 1)
    mix(0, 0, 0, head, 0, ahead, cols)
    refill(0, 0)
    for k in range(1, ns):
        send_column(k)
    loaded(0, 1)
    mix(1, 0, 1, head, 1)
    refill(0, 1)
    exchange(head, 1)
    collect(first_sums, 0)
    divide(0, 0, 0, first_sums, 0, 0, ahead, 4 * ROWS)
    tell(first_sums, 0)
    both_ways(lambda step: send_part(lead, step))
    if experts > 1:
        loaded(1, 0)
        mix(2, 1, 2, tail, 0)
        refill(1, 0)
    collect(head, 1)
    divide(0, 0, 0, head, 0, ahead, cols)
    both_ways(lambda step: send_part(follow, step))
    tell(head, 1)
    local_copy(0, 0).start()
    if experts > 1:
        loaded(1, 1)
        mix(3, 1, 3, tail, 1)
        refill(1, 1)

        def more(e, carry):
            for which in range(2):
                loaded(e, which)
                mix(2 * e + which, e, slot_of(e, which), tail, 2 * (e - 1) + which)
                refill(e, which)
            return carry

        lax.fori_loop(2, experts, more, 0)
        exchange(tail, 2)
    finish(0, 1, head, 1)
    if experts > 1:
        collect(tail, 2)
        finish(1, 0, tail, 0)
        tell(tail, 2)
        finish(1, 1, tail, 1)

        def rest(e, carry):
            for which in range(2):
                finish(e, which, tail, 2 * (e - 1) + which)
            return carry

        lax.fori_loop(2, experts, rest, 0)

    for step in (-1, 1):
        send_last(step, 0)

    @pl.when(inner)
    def _():
        pltpu.make_async_copy(narrow.at[n - 1], bundle_ref.at[slot_at(z, z)], local_sem.at[0]).start()

    @pl.when(outer)
    def _():
        local_copy(experts - 1, 1).start()

    for which, ref in enumerate((sg_ref, su_ref)):
        pltpu.make_async_copy(scale.at[which], ref, own_sem.at[1]).start()

    wait_for(column.at[pl.ds(0, ns - 1)], column_sem.at[1])
    own_table.start()
    lax.fori_loop(1, ne, send_table, 0)

    def each(step):
        def one(e, carry):
            step(e, 2)
            return carry

        lax.fori_loop(0, experts - 1, one, 0)
        step(experts - 1, 1)

    def land(e, count, d):
        pl.when(z >= d)(lambda: wait_for(pieces(count), recv_sem.at[z - d, e]))
        pl.when(z + d < ns)(lambda: wait_for(pieces(count), recv_sem.at[z + d, e]))

    def goes_on(step, d):
        return (z + d < ns) & (z > 0) if step < 0 else (z >= d) & (z < ns - 1)

    for d in range(1, ns - 1):
        def pass_on(e, count, d=d):
            land(e, count, d)
            for step in (-1, 1):
                @pl.when(goes_on(step, d))
                def _():
                    for which in range(count):
                        send_on(e, which, step, d)

        each(pass_on)

        @pl.when(inner)
        def _():
            pl.when(z >= d)(lambda: wait_for(pieces(1), last_recv.at[z - d]))
            pl.when(z + d < ns)(lambda: wait_for(pieces(1), last_recv.at[z + d]))

        for step in (-1, 1):
            send_last(step, d)

    wait_for(pieces(n), local_sem.at[0])
    wait_for(scale, own_sem.at[1])
    own_table.wait()
    for i in range(2):
        wait_for(table_ref.at[pl.ds(0, ne - 1)], table_sem.at[i])
    wait_for(column.at[pl.ds(0, ns - 1)], column_sem.at[0])
    for group, part in enumerate((first_sums, head, tail)[: 3 if experts > 1 else 2]):
        exchanged(part, group)
    for d in range(ns - 1):
        for step in (-1, 1):
            pl.when(last_goes(step, d))(lambda: wait_for(pieces(1), last_sent(step, d)))
    for d in range(ns - 1):
        for step in (-1, 1):
            pl.when(goes_on(step, d))(lambda: wait_for(pieces(n - 1), sent(step, d)))
    each(lambda e, count: land(e, count, ns - 1))


def shard_in(slot, ns):
    z = lax.axis_index("shard")
    return jnp.where(z < ns // 2, slot + 1, slot)


def move_kernel(src_ref, dst_ref):
    dst_ref[...] = src_ref[...]


def move(raw):
    block = pl.BlockSpec((1,) + raw.shape[1:], lambda i: (i, 0, 0))
    return pl.pallas_call(
        move_kernel,
        grid=(raw.shape[0],),
        out_shape=jax.ShapeDtypeStruct(raw.shape, raw.dtype),
        in_specs=[block],
        out_specs=block,
        compiler_params=pltpu.CompilerParams(vmem_limit_bytes=32 * 1024 * 1024),
        cost_estimate=pl.CostEstimate(flops=0, bytes_accessed=2 * raw.size * raw.dtype.itemsize, transcendentals=0),
    )(raw)


def move_all_kernel(ns, rows, raw_ref, bundle_ref, *refs):
    count = len(refs) // 2
    dst_ref, smalls, copies = refs[count], refs[:count], refs[count + 1 :]
    dst_ref[...] = raw_ref[...]
    z = lax.axis_index("shard")

    @pl.when(pl.program_id(0) == 0)
    def _():
        for small, copy in zip(smalls, copies):
            copy[...] = small[...]

    @pl.when((pl.program_id(0) == pl.num_programs(0) - 1) & (z > 0) & (z < ns - 1))
    def _():
        for slot in range(ns - 1):
            at = pl.multiple_of(shard_in(slot, ns) * rows, rows)
            dst_ref[0, pl.ds(at, rows), :] = bundle_ref[slot]


def move_all(ns, raw, bundle, smalls):
    block = pl.BlockSpec((1,) + raw.shape[1:], lambda i: (i, 0, 0))

    def whole(x):
        return pl.BlockSpec(x.shape, lambda i: (0,) * x.ndim)

    return pl.pallas_call(
        functools.partial(move_all_kernel, ns, bundle.shape[1]),
        grid=(raw.shape[0],),
        out_shape=[jax.ShapeDtypeStruct(x.shape, x.dtype) for x in (raw, *smalls)],
        in_specs=[block, whole(bundle)] + [whole(x) for x in smalls],
        out_specs=[block] + [whole(x) for x in smalls],
        compiler_params=pltpu.CompilerParams(vmem_limit_bytes=40 * 1024 * 1024),
        cost_estimate=pl.CostEstimate(flops=0, bytes_accessed=2 * raw.size * raw.dtype.itemsize, transcendentals=0),
    )(raw, bundle, *smalls)


def fill_kernel(ns, pieces_ref, whole_ref, out_ref, sem):
    rows = pieces_ref.shape[1]
    z = lax.axis_index("shard")

    @pl.when((z == 0) | (z == ns - 1))
    def _():
        stores = []
        for slot in range(ns - 1):
            at = pl.multiple_of(shard_in(slot, ns) * rows, rows)
            spot = out_ref.at[out_ref.shape[0] - 1, pl.ds(at, rows), :]
            stores.append(pltpu.make_async_copy(pieces_ref.at[slot], spot, sem.at[slot]))
        for store in stores:
            store.start()
        for store in stores:
            store.wait()


def fill(ns, pieces, whole):
    anywhere = pl.BlockSpec(memory_space=pl.ANY)
    return pl.pallas_call(
        functools.partial(fill_kernel, ns),
        out_shape=jax.ShapeDtypeStruct(whole.shape, whole.dtype),
        in_specs=[pl.BlockSpec(memory_space=pltpu.VMEM), anywhere],
        out_specs=anywhere,
        input_output_aliases={1: 0},
        scratch_shapes=[pltpu.SemaphoreType.DMA((ns - 1,))],
        compiler_params=pltpu.CompilerParams(vmem_limit_bytes=32 * 1024 * 1024),
    )(pieces, whole)


def solution(mesh):
    ns, ne = mesh.shape["shard"], mesh.shape["expert"]
    assert ns >= 4

    def per_device(w_gate, avg_gate, w_up, avg_up, mix_share, router_weight, router_gain):
        experts, rows, cols = w_gate.shape
        n = 2 * experts
        ahead = max(cols // HEAD_PARTS // 128, 1) * 128
        dma = pltpu.SemaphoreType.DMA
        f32, bf16 = jnp.float32, jnp.bfloat16
        anywhere = pl.BlockSpec(memory_space=pl.ANY)
        serve = jax.ShapeDtypeStruct((experts, ns * rows, cols), bf16)
        scale = jax.ShapeDtypeStruct((experts, cols), f32)
        bundle = jax.ShapeDtypeStruct((ns - 1, rows, cols), bf16)
        table = jax.ShapeDtypeStruct((ne, ns, experts, rows), bf16)
        raw_gate, raw_up, scale_gate, scale_up, bundle, table = pl.pallas_call(
            functools.partial(kernel, ns, ne, experts, rows, cols, ahead),
            out_shape=(serve, serve, scale, scale, bundle, table),
            in_specs=[anywhere] * 7,
            out_specs=(anywhere,) * 6,
            scratch_shapes=[
                pltpu.VMEM((n, rows, cols), f32),
                pltpu.VMEM((SLOTS, rows, cols), f32),
                pltpu.VMEM((n, rows, cols), bf16),
                pltpu.VMEM((ns + 1, 1, ahead), f32),
                pltpu.VMEM((ns + 1, 2, cols), f32),
                pltpu.VMEM((ns + 1, max(n - 2, 1), cols), f32),
                pltpu.VMEM((2, experts, cols), f32),
                pltpu.SMEM((experts,), f32),
                pltpu.VMEM((experts, rows), f32),
                pltpu.VMEM((1, rows), f32),
                pltpu.VMEM((ns, experts, rows), bf16),
                dma((SLOTS,)),
                dma((1,)),
                dma((3,)),
                dma((1,)),
                dma((ns, experts)),
                dma((ns,)),
                dma((2, ns - 1)),
                dma((2, ns - 1)),
                dma((3, 4)),
                dma((2,)),
                dma((2,)),
                dma((2,)),
            ],
            compiler_params=pltpu.CompilerParams(
                collective_id=0, has_side_effects=True, vmem_limit_bytes=62 * 1024 * 1024
            ),
        )(mix_share, w_gate, avg_gate, w_up, avg_up, router_weight.T, router_gain.reshape(1, rows))
        pieces = lax.ppermute(bundle, "shard", [(1, 0), (ns - 2, ns - 1)])
        serve_gate = move(raw_gate)
        whole, scale_gate, scale_up, table = move_all(ns, raw_up, bundle, (scale_gate, scale_up, table))
        serve_up = fill(ns, pieces, whole)
        serve_router = table.transpose(1, 3, 0, 2).reshape(ns * rows, ne * experts)
        return serve_gate, serve_up, scale_gate, scale_up, serve_router

    return jax.shard_map(
        per_device,
        mesh=mesh,
        in_specs=(
            P("expert", "shard", None),
            P("expert", "shard", None),
            P("expert", "shard", None),
            P("expert", "shard", None),
            P("expert"),
            P("shard", "expert"),
            P("shard"),
        ),
        out_specs=(
            P("expert", None, None),
            P("expert", None, None),
            P("expert", None),
            P("expert", None),
            P(),
        ),
        check_vma=False,
    )
```

time: 1100 us -> 1100 us (level)
  no operation moved by 1% of the time
where the time goes in v2:
time: 1100 us
  Pallas kernels  1070 us (97%)
  waiting for transfers between devices  22 us (2%)
    pallas_call x1, Pallas kernels, per_device(): pl.pallas_call(functools.partial(kernel, ns, ne, experts, rows, cols, ahe...  1020 us
    pallas_call x1, Pallas kernels, move(): pl.pallas_call(move_kernel, grid=(raw.shape[0],), out_shape=jax.ShapeDtyp...  23.5 us
    pallas_call x1, Pallas kernels, move_all(): pl.pallas_call(functools.partial(move_all_kernel, ns, bundle.shape[1]), g...  22.6 us
    ppermute x1, waiting for transfers between devices, per_device(): pieces = lax.ppermute(bundle, 'shard', [(1, 0), (ns - 2, ns - 1)])  22 us
  transfers between devices with their start and end apart: 1, of which 1 were waited for; matrix products, arithmetic and copies ran while one was open for 0% of the time, Pallas kernels for 4%

profile of v2, /device:TPU:0, one launch (start us, length us, event | category | flops | bytes accessed | tf_op | source)
XLA Modules:
  0.0 1095.4 jit_solution(15583968710231020225)
XLA Ops:
  0.6 1023.6 %shard_map.110 = (bf16[8,2048,1024]{2,1,0:T(8,128)(2,1)}, bf16[8,2048,1024]{2,1,0:T(8,128)(2,1)}, f32[8,1024]{1,0:T(8,128)}, f32[8,1024]{1,0:T(8,128)}, bf16[3,5...) custom-call(f32[8]{0:T(128)} %mix_ref.1, f32[8,512,1024]{2,1,0:T(8,128)} %wg_ref.1, f32[8,512,1024]{2,1,0:T(8,128)} %ag_ref.1, ...), custom_call_target="tpu_custom_call" | custom-call | tf_op jit(solution)/shard_map/pallas_call | solution.py:460
  1024.2 1.3 collective-permute-start
  1025.5 0.0 copy-start
  1025.5 0.0 copy-start.1
  1025.5 0.0 copy-start.2
  1025.5 0.0 copy-start.3
  1025.6 23.5 %shard_map.111 = bf16[8,2048,1024]{2,1,0:T(8,128)(2,1)} custom-call(bf16[8,2048,1024]{2,1,0:T(8,128)(2,1)} %get-tuple-element.15.src_ref), custom_call_target="tpu_custom_call" | custom-call | bytes 67108864 | tf_op jit(solution)/shard_map/pallas_call | solution.py:369
  1049.0 0.0 copy-done
  1049.0 0.0 copy-done.1
  1049.0 0.0 copy-done.2
  1049.0 0.0 copy-done.3
  1049.1 22.6 %shard_map.112 = (bf16[8,2048,1024]{2,1,0:T(8,128)(2,1)}, f32[8,1024]{1,0:T(8,128)}, f32[8,1024]{1,0:T(8,128)}, bf16[8,4,8,512]{3,2,1,0:T(8,128)(2,1)}) custom-call(bf16[8,2048,1024]{2,1,0:T(8,128)(2,1)} %get-tuple-element.17.raw_ref, bf16[3,512,1024]{2,1,0:T(8,128)(2,1)S(1)} %copy-done, f32[8,1024]{1,0:T(8,128)S(1)} %copy-done.2, f32[8,1024]{1,0:T(8,128)S(1)} %copy-done.3, ...), custom_call_target="tpu_custom_call" | custom-call | bytes 67108864 | tf_op jit(solution)/shard_map/pallas_call | solution.py:404
  1071.7 22.0 %collective-permute-done.pieces_ref = bf16[3,512,1024]{2,1,0:T(8,128)(2,1)S(1)} collective-permute-done((bf16[3,512,1024]{2,1,0:T(8,128)(2,1)}, bf16[3,512,1024]{2,1,0:T(8,128)(2,1)S(1)}, u32[]{:S(2)}, u32[]{:S(2)}) %collective-permute-start) | collective-permute-done | bytes 3145760 | tf_op jit(solution)/shard_map/ppermute | solution.py:494
  1093.7 1.7 shard_map.113
Async XLA Ops:
  1024.2 69.5 %collective-permute-start = (bf16[3,512,1024]{2,1,0:T(8,128)(2,1)}, bf16[3,512,1024]{2,1,0:T(8,128)(2,1)S(1)}, u32[]{:S(2)}, u32[]{:S(2)}) collective-permute-start(bf16[3,512,1024]{2,1,0:T(8,128)(2,1)} %get-tuple-element.16.bundle_ref), channel_id=1, source_target_pairs={{1,0},{2,3},{5,4},{6,7},{9,8},{10,11},{13,12},{14,15},{17,16},{18,... | collective-permute-start | bytes 9437192 | tf_op jit(solution)/shard_map/ppermute | solution.py:494
  1025.5 23.5 %copy-start = (bf16[3,512,1024]{2,1,0:T(8,128)(2,1)S(1)}, bf16[3,512,1024]{2,1,0:T(8,128)(2,1)}, u32[]{:S(2)}) copy-start(bf16[3,512,1024]{2,1,0:T(8,128)(2,1)} %get-tuple-element.16.bundle_ref) | copy-start | bytes 9437188
  1025.5 23.5 %copy-start.1 = (bf16[8,4,8,512]{3,2,1,0:T(8,128)(2,1)S(1)}, bf16[8,4,8,512]{3,2,1,0:T(8,128)(2,1)}, u32[]{:S(2)}) copy-start(bf16[8,4,8,512]{3,2,1,0:T(8,128)(2,1)} %get-tuple-element.20.refs_2_) | copy-start | bytes 786436
  1025.5 23.5 %copy-start.2 = (f32[8,1024]{1,0:T(8,128)S(1)}, f32[8,1024]{1,0:T(8,128)}, u32[]{:S(2)}) copy-start(f32[8,1024]{1,0:T(8,128)} %get-tuple-element.18.refs_0_) | copy-start | bytes 98308
  1025.5 23.5 %copy-start.3 = (f32[8,1024]{1,0:T(8,128)S(1)}, f32[8,1024]{1,0:T(8,128)}, u32[]{:S(2)}) copy-start(f32[8,1024]{1,0:T(8,128)} %get-tuple-element.19.refs_1_) | copy-start | bytes 98308

commit v3 on v2

--- a/solution.py
+++ b/solution.py
@@ -11,15 +11,16 @@
 SLOTS = 4
 ROWS = 16
 HEAD_PARTS = 4
+EDGE = 128
 
 
 def kernel(
-    ns, ne, experts, rows, cols, ahead,
+    ns, ne, experts, rows, cols, ahead, top, splits,
     mix_ref, wg_ref, ag_ref, wu_ref, au_ref, router_ref, gain_ref,
-    og_ref, ou_ref, sg_ref, su_ref, bundle_ref, table_ref,
-    fresh, other, narrow, first_sums, head, tail, scale, mix_s, weight, gain, column,
+    og_ref, ou_ref, sg_ref, su_ref, big_ref, small_ref, table_ref,
+    fresh, other, narrow, first_sums, head, tail, scale, mix_s, weight, gain, column, edge32, edge16,
     load_sem, first_sem, small_sem, local_sem, recv_sem, last_recv, send_sem, last_send,
-    sums_sem, column_sem, table_sem, own_sem,
+    sums_sem, column_sem, table_sem, own_sem, edge_sem,
 ):
     z, me = lax.axis_index("shard"), lax.axis_index("expert")
     n = 2 * experts
@@ -28,6 +29,12 @@
     lead, follow = pl.ds(0, ahead), pl.ds(ahead, cols - ahead)
     inner = (z > 0) & (z < ns - 1)
     outer = jnp.logical_not(inner)
+    near = jnp.where(z == 0, 1, ns - 2)
+    edge_rows = rows - top * EDGE // cols
+    bundles = tuple(zip((big_ref, small_ref), splits))
+
+    def outward(step):
+        return z == 1 if step < 0 else z == ns - 2
 
     def load_part(part, sem):
         pltpu.make_async_copy(wg_ref.at[0, :, part], fresh.at[0, :, part], sem).start()
@@ -92,8 +99,45 @@
         src = narrow.at[2 * e + which] if d == 0 else spot
         hop(src, spot, step, sent(step, d), recv_sem.at[j, e]).start()
 
-    def send_part(part, step):
-        hop(narrow.at[0, :, part], place(0, 0, z).at[:, part], step, sent(step, 0), recv_sem.at[z, 0]).start()
+    def send_block(r, c, step, send):
+        hop(narrow.at[0, r, c], place(0, 0, z).at[r, c], step, send, recv_sem.at[z, 0]).start()
+
+    def send_edge(step):
+        @pl.when(outward(step))
+        def _():
+            hop(fresh.at[0, pl.ds(0, top), pl.ds(0, EDGE)], edge32, step, edge_sem.at[0], edge_sem.at[1]).start()
+
+    def send_lead(step):
+        @pl.when(outward(step))
+        def _():
+            if ahead > EDGE:
+                send_block(pl.ds(0, rows), pl.ds(EDGE, ahead - EDGE), step, edge_sem.at[2])
+            send_block(pl.ds(top, rows - top), pl.ds(0, EDGE), step, edge_sem.at[2])
+
+        @pl.when(jnp.logical_not(outward(step)))
+        def _():
+            send_block(pl.ds(0, rows), lead, step, sent(step, 0))
+
+    def send_follow(step):
+        @pl.when(outward(step))
+        def _():
+            send_block(pl.ds(0, rows), follow, step, edge_sem.at[2])
+
+        @pl.when(jnp.logical_not(outward(step)))
+        def _():
+            send_block(pl.ds(0, rows), follow, step, sent(step, 0))
+
+    def divide_edge():
+        wait_for(edge32, edge_sem.at[1])
+        wide = jnp.broadcast_to(scale[0, pl.ds(0, 1), pl.ds(0, EDGE)], (8, EDGE))
+        wide = jnp.concatenate([wide] * (ROWS // 8), axis=0)
+
+        def step(i, carry):
+            r = pl.ds(pl.multiple_of(i * ROWS, ROWS), ROWS)
+            edge16[r, :] = (edge32[r, :] / wide).astype(jnp.bfloat16)
+            return carry
+
+        lax.fori_loop(0, top // ROWS, step, 0)
 
     def pieces(count):
         return narrow.at[pl.ds(0, count)]
@@ -125,9 +169,12 @@
 
                 @pl.when(fits)
                 def _():
-                    src = narrow.at[n - 1] if d == 0 else spot if from_plain else bundle_ref.at[slot_at(z, j)]
-                    dst = spot if to_plain else bundle_ref.at[slot_at(z + step, j)]
-                    hop(src, dst, step, last_sent(step, d), last_recv.at[j]).start()
+                    for ref, (lo, size) in bundles:
+                        part = pl.ds(lo, size)
+                        plain = spot.at[part]
+                        src = narrow.at[n - 1, part] if d == 0 else plain if from_plain else ref.at[slot_at(z, j)]
+                        dst = plain if to_plain else ref.at[slot_at(z + step, j)]
+                        hop(src, dst, step, last_sent(step, d), last_recv.at[j]).start()
 
     def block_of(part, device, group, send, recv, slot):
         return pltpu.make_async_remote_copy(
@@ -230,6 +277,8 @@
     mix(0, 0, 0, first_sums, 0, 0, ahead, 4 * ROWS)
     pl.semaphore_wait(barrier, ns - 1 + ne - 1)
     exchange(first_sums, 0)
+    for step in (-1, 1):
+        send_edge(step)
     get_weight.wait()
     get_gain.wait()
     column[z] = (weight[...] * gain[...]).astype(jnp.bfloat16)
@@ -248,14 +297,14 @@
     collect(first_sums, 0)
     divide(0, 0, 0, first_sums, 0, 0, ahead, 4 * ROWS)
     tell(first_sums, 0)
-    both_ways(lambda step: send_part(lead, step))
+    both_ways(send_lead)
     if experts > 1:
         loaded(1, 0)
         mix(2, 1, 2, tail, 0)
         refill(1, 0)
     collect(head, 1)
     divide(0, 0, 0, head, 0, ahead, cols)
-    both_ways(lambda step: send_part(follow, step))
+    both_ways(send_follow)
     tell(head, 1)
     local_copy(0, 0).start()
     if experts > 1:
@@ -291,11 +340,14 @@
 
     @pl.when(inner)
     def _():
-        pltpu.make_async_copy(narrow.at[n - 1], bundle_ref.at[slot_at(z, z)], local_sem.at[0]).start()
+        for ref, (lo, size) in bundles:
+            own = narrow.at[n - 1, pl.ds(lo, size)]
+            pltpu.make_async_copy(own, ref.at[slot_at(z, z)], local_sem.at[0]).start()
 
     @pl.when(outer)
     def _():
         local_copy(experts - 1, 1).start()
+        divide_edge()
 
     for which, ref in enumerate((sg_ref, su_ref)):
         pltpu.make_async_copy(scale.at[which], ref, own_sem.at[1]).start()
@@ -303,18 +355,29 @@
     wait_for(column.at[pl.ds(0, ns - 1)], column_sem.at[1])
     own_table.start()
     lax.fori_loop(1, ne, send_table, 0)
+
+    @pl.when(outer)
+    def _():
+        spot = place(0, 0, near).at[pl.ds(0, top), pl.ds(0, EDGE)]
+        pltpu.make_async_copy(edge16, spot, edge_sem.at[3]).start()
 
     def each(step):
         def one(e, carry):
             step(e, 2)
             return carry
 
-        lax.fori_loop(0, experts - 1, one, 0)
+        if experts > 1:
+            step(0, 2)
+            lax.fori_loop(1, experts - 1, one, 0)
         step(experts - 1, 1)
 
     def land(e, count, d):
-        pl.when(z >= d)(lambda: wait_for(pieces(count), recv_sem.at[z - d, e]))
-        pl.when(z + d < ns)(lambda: wait_for(pieces(count), recv_sem.at[z + d, e]))
+        for fits, j in ((z >= d, z - d), (z + d < ns, z + d)):
+            if isinstance(e, int) and e == 0 and d == 1:
+                short = og_ref.at[0, pl.ds(0, (count - 1) * rows + edge_rows), :]
+                pl.when(fits & outer)(lambda: wait_for(short, recv_sem.at[j, 0]))
+                fits = fits & inner
+            pl.when(fits)(lambda: wait_for(pieces(count), recv_sem.at[j, e]))
 
     def goes_on(step, d):
         return (z + d < ns) & (z > 0) if step < 0 else (z >= d) & (z < ns - 1)
@@ -349,9 +412,23 @@
     for d in range(ns - 1):
         for step in (-1, 1):
             pl.when(last_goes(step, d))(lambda: wait_for(pieces(1), last_sent(step, d)))
+    @pl.when(outer)
+    def _():
+        wait_for(edge16, edge_sem.at[3])
+
     for d in range(ns - 1):
         for step in (-1, 1):
-            pl.when(goes_on(step, d))(lambda: wait_for(pieces(n - 1), sent(step, d)))
+            fits = goes_on(step, d)
+            if d == 0:
+                @pl.when(outward(step))
+                def _():
+                    wait_for(edge32, edge_sem.at[0])
+                    wait_for(narrow.at[0, pl.ds(0, edge_rows)], edge_sem.at[2])
+                    if n > 2:
+                        wait_for(pieces(n - 2), sent(step, 0))
+
+                fits = fits & jnp.logical_not(outward(step))
+            pl.when(fits)(lambda: wait_for(pieces(n - 1), sent(step, d)))
     each(lambda e, count: land(e, count, ns - 1))
 
 
@@ -377,7 +454,7 @@
     )(raw)
 
 
-def move_all_kernel(ns, rows, raw_ref, bundle_ref, *refs):
+def move_all_kernel(ns, rows, splits, raw_ref, big_ref, small_ref, *refs):
     count = len(refs) // 2
     dst_ref, smalls, copies = refs[count], refs[:count], refs[count + 1 :]
     dst_ref[...] = raw_ref[...]
@@ -390,38 +467,38 @@
 
     @pl.when((pl.program_id(0) == pl.num_programs(0) - 1) & (z > 0) & (z < ns - 1))
     def _():
-        for slot in range(ns - 1):
-            at = pl.multiple_of(shard_in(slot, ns) * rows, rows)
-            dst_ref[0, pl.ds(at, rows), :] = bundle_ref[slot]
-
-
-def move_all(ns, raw, bundle, smalls):
+        for ref, (lo, size) in zip((big_ref, small_ref), splits):
+            for slot in range(ns - 1):
+                at = pl.multiple_of(shard_in(slot, ns) * rows + lo, 16)
+                dst_ref[0, pl.ds(at, size), :] = ref[slot]
+
+
+def move_all(ns, rows, splits, raw, bundles, smalls):
     block = pl.BlockSpec((1,) + raw.shape[1:], lambda i: (i, 0, 0))
 
     def whole(x):
         return pl.BlockSpec(x.shape, lambda i: (0,) * x.ndim)
 
     return pl.pallas_call(
-        functools.partial(move_all_kernel, ns, bundle.shape[1]),
+        functools.partial(move_all_kernel, ns, rows, splits),
         grid=(raw.shape[0],),
         out_shape=[jax.ShapeDtypeStruct(x.shape, x.dtype) for x in (raw, *smalls)],
-        in_specs=[block, whole(bundle)] + [whole(x) for x in smalls],
+        in_specs=[block] + [whole(x) for x in (*bundles, *smalls)],
         out_specs=[block] + [whole(x) for x in smalls],
         compiler_params=pltpu.CompilerParams(vmem_limit_bytes=40 * 1024 * 1024),
         cost_estimate=pl.CostEstimate(flops=0, bytes_accessed=2 * raw.size * raw.dtype.itemsize, transcendentals=0),
-    )(raw, bundle, *smalls)
-
-
-def fill_kernel(ns, pieces_ref, whole_ref, out_ref, sem):
-    rows = pieces_ref.shape[1]
+    )(raw, *bundles, *smalls)
+
+
+def fill_kernel(ns, rows, lo, pieces_ref, whole_ref, out_ref, sem):
     z = lax.axis_index("shard")
 
     @pl.when((z == 0) | (z == ns - 1))
     def _():
         stores = []
         for slot in range(ns - 1):
-            at = pl.multiple_of(shard_in(slot, ns) * rows, rows)
-            spot = out_ref.at[out_ref.shape[0] - 1, pl.ds(at, rows), :]
+            at = pl.multiple_of(shard_in(slot, ns) * rows + lo, 16)
+            spot = out_ref.at[out_ref.shape[0] - 1, pl.ds(at, pieces_ref.shape[1]), :]
             stores.append(pltpu.make_async_copy(pieces_ref.at[slot], spot, sem.at[slot]))
         for store in stores:
             store.start()
@@ -429,16 +506,18 @@
             store.wait()
 
 
-def fill(ns, pieces, whole):
+def fill(ns, rows, lo, pieces, whole):
     anywhere = pl.BlockSpec(memory_space=pl.ANY)
+    size = 2 * pieces.size * pieces.dtype.itemsize
     return pl.pallas_call(
-        functools.partial(fill_kernel, ns),
+        functools.partial(fill_kernel, ns, rows, lo),
         out_shape=jax.ShapeDtypeStruct(whole.shape, whole.dtype),
         in_specs=[pl.BlockSpec(memory_space=pltpu.VMEM), anywhere],
         out_specs=anywhere,
         input_output_aliases={1: 0},
         scratch_shapes=[pltpu.SemaphoreType.DMA((ns - 1,))],
         compiler_params=pltpu.CompilerParams(vmem_limit_bytes=32 * 1024 * 1024),
+        cost_estimate=pl.CostEstimate(flops=0, bytes_accessed=size, transcendentals=0),
     )(pieces, whole)
 
 
@@ -450,18 +529,22 @@
         experts, rows, cols = w_gate.shape
         n = 2 * experts
         ahead = max(cols // HEAD_PARTS // 128, 1) * 128
+        top = rows * 3 // 4 // 16 * 16
+        assert top * EDGE % cols == 0
+        large = rows * 7 // 8 // 16 * 16
+        splits = ((0, large), (large, rows - large))
         dma = pltpu.SemaphoreType.DMA
         f32, bf16 = jnp.float32, jnp.bfloat16
         anywhere = pl.BlockSpec(memory_space=pl.ANY)
         serve = jax.ShapeDtypeStruct((experts, ns * rows, cols), bf16)
         scale = jax.ShapeDtypeStruct((experts, cols), f32)
-        bundle = jax.ShapeDtypeStruct((ns - 1, rows, cols), bf16)
+        bundles = tuple(jax.ShapeDtypeStruct((ns - 1, size, cols), bf16) for _, size in splits)
         table = jax.ShapeDtypeStruct((ne, ns, experts, rows), bf16)
-        raw_gate, raw_up, scale_gate, scale_up, bundle, table = pl.pallas_call(
-            functools.partial(kernel, ns, ne, experts, rows, cols, ahead),
-            out_shape=(serve, serve, scale, scale, bundle, table),
+        raw_gate, raw_up, scale_gate, scale_up, *bundles, table = pl.pallas_call(
+            functools.partial(kernel, ns, ne, experts, rows, cols, ahead, top, splits),
+            out_shape=(serve, serve, scale, scale, *bundles, table),
             in_specs=[anywhere] * 7,
-            out_specs=(anywhere,) * 6,
+            out_specs=(anywhere,) * 7,
             scratch_shapes=[
                 pltpu.VMEM((n, rows, cols), f32),
                 pltpu.VMEM((SLOTS, rows, cols), f32),
@@ -474,6 +557,8 @@
                 pltpu.VMEM((experts, rows), f32),
                 pltpu.VMEM((1, rows), f32),
                 pltpu.VMEM((ns, experts, rows), bf16),
+                pltpu.VMEM((top, EDGE), f32),
+                pltpu.VMEM((top, EDGE), bf16),
                 dma((SLOTS,)),
                 dma((1,)),
                 dma((3,)),
@@ -486,15 +571,18 @@
                 dma((2,)),
                 dma((2,)),
                 dma((2,)),
+                dma((4,)),
             ],
             compiler_params=pltpu.CompilerParams(
                 collective_id=0, has_side_effects=True, vmem_limit_bytes=62 * 1024 * 1024
             ),
         )(mix_share, w_gate, avg_gate, w_up, avg_up, router_weight.T, router_gain.reshape(1, rows))
-        pieces = lax.ppermute(bundle, "shard", [(1, 0), (ns - 2, ns - 1)])
+        pieces = [lax.ppermute(bundle, "shard", [(1, 0), (ns - 2, ns - 1)]) for bundle in bundles]
         serve_gate = move(raw_gate)
-        whole, scale_gate, scale_up, table = move_all(ns, raw_up, bundle, (scale_gate, scale_up, table))
-        serve_up = fill(ns, pieces, whole)
+        smalls = (scale_gate, scale_up, table)
+        serve_up, scale_gate, scale_up, table = move_all(ns, rows, splits, raw_up, bundles, smalls)
+        for (lo, _), piece in zip(splits, pieces):
+            serve_up = fill(ns, rows, lo, piece, serve_up)
         serve_router = table.transpose(1, 3, 0, 2).reshape(ns * rows, ne * experts)
         return serve_gate, serve_up, scale_gate, scale_up, serve_router
 

time: 1100 us -> 1090 us (level)
    ppermute x1 -> x2, waiting for transfers between devices: 22 us -> 18.9 us  [per_device(): lax.ppermute(bundle, 'shard', [(1, 0), (ns - 2, ns - 1)])]
    pallas_call x2 -> x3, Pallas kernels: 24.3 us -> 24.9 us  [the longest x1 22.6 us: move_all(): pl.pallas_call(functools.partial(move_all_kernel, ns, rows, splits), grid...]
  transfers between devices with their start and end apart: 1 -> 2, of which waited for: 1 -> 2; matrix products, arithmetic and copies ran while one was open for 0% -> 0% of each run, Pallas kernels for 4% -> 4%
where the time goes in v3:
time: 1090 us
  Pallas kernels  1070 us (98%)
  waiting for transfers between devices  18.9 us (2%)
    pallas_call x1, Pallas kernels, per_device(): pl.pallas_call(functools.partial(kernel, ns, ne, experts, rows, cols, ahe...  1020 us
    pallas_call x1, Pallas kernels, move(): pl.pallas_call(move_kernel, grid=(raw.shape[0],), out_shape=jax.ShapeDtyp...  23.5 us
    pallas_call x1, Pallas kernels, move_all(): pl.pallas_call(functools.partial(move_all_kernel, ns, rows, splits), grid...  22.6 us
  transfers between devices with their start and end apart: 2, of which 2 were waited for; matrix products, arithmetic and copies ran while one was open for 0% of the time, Pallas kernels for 4%

profile of v3, /device:TPU:0, one launch (start us, length us, event | category | flops | bytes accessed | tf_op | source)
XLA Modules:
  0.0 1093.5 jit_solution(12269999959373550017)
XLA Ops:
  0.6 1022.8 %shard_map.110 = (bf16[8,2048,1024]{2,1,0:T(8,128)(2,1)}, bf16[8,2048,1024]{2,1,0:T(8,128)(2,1)}, f32[8,1024]{1,0:T(8,128)}, f32[8,1024]{1,0:T(8,128)}, bf16[3,4...) custom-call(f32[8]{0:T(128)} %mix_ref.1, f32[8,512,1024]{2,1,0:T(8,128)} %wg_ref.1, ...), custom_call_target="tpu_custom_call" | custom-call | tf_op jit(solution)/shard_map/pallas_call | solution.py:543
  1023.4 1.3 collective-permute-start.1
  1024.7 1.3 collective-permute-start
  1026.0 0.0 copy-start
  1026.0 0.0 copy-start.1
  1026.1 0.0 copy-start.2
  1026.1 0.0 copy-start.3
  1026.1 0.0 copy-start.4
  1026.1 23.5 %shard_map.111 = bf16[8,2048,1024]{2,1,0:T(8,128)(2,1)} custom-call(bf16[8,2048,1024]{2,1,0:T(8,128)(2,1)} %get-tuple-element.16.src_ref), custom_call_target="tpu_custom_call" | custom-call | bytes 67108864 | tf_op jit(solution)/shard_map/pallas_call | solution.py:446
  1049.6 0.0 copy-done
  1049.6 0.0 copy-done.1
  1049.6 0.0 copy-done.2
  1049.6 0.0 copy-done.3
  1049.6 0.0 copy-done.4
  1049.6 22.6 %shard_map.112 = (bf16[8,2048,1024]{2,1,0:T(8,128)(2,1)}, f32[8,1024]{1,0:T(8,128)}, f32[8,1024]{1,0:T(8,128)}, bf16[8,4,8,512]{3,2,1,0:T(8,128)(2,1)}) custom-call(bf16[8,2048,1024]{2,1,0:T(8,128)(2,1)} %get-tuple-element.19.raw_ref, bf16[3,448,1024]{2,1,0:T(8,128)(2,1)S(1)} %copy-done, bf16[3,64,1024]{2,1,0:T(8,128)(2,1)S(1)} %copy-done.1, ...), custom_call_target="tpu_custom_call" | custom-call | bytes 67108864 | tf_op jit(solution)/shard_map/pallas_call | solution.py:482
  1072.2 15.9 %collective-permute-done.1.pieces_ref = bf16[3,448,1024]{2,1,0:T(8,128)(2,1)S(1)} collective-permute-done((bf16[3,448,1024]{2,1,0:T(8,128)(2,1)}, bf16[3,448,1024]{2,1,0:T(8,128)(2,1)S(1)}, u32[]{:S(2)}, u32[]{:S(2)}) %collective-permute-start.1) | collective-permute-done | bytes 2752544 | tf_op jit(solution)/shard_map/ppermute | solution.py:580
  1088.1 1.6 shard_map.113.whole_ref
  1089.6 3.0 collective-permute-done.pieces_ref
  1092.7 0.8 shard_map.114
Async XLA Ops:
  1023.4 64.6 %collective-permute-start.1 = (bf16[3,448,1024]{2,1,0:T(8,128)(2,1)}, bf16[3,448,1024]{2,1,0:T(8,128)(2,1)S(1)}, u32[]{:S(2)}, u32[]{:S(2)}) collective-permute-start(bf16[3,448,1024]{2,1,0:T(8,128)(2,1)} %get-tuple-element.18.big_ref), channel_id=1, source_target_pairs={{1,0},{2,3},{5,4},{6,7},{9,8},{10,11},{13,12},{14,15},{17,16},{18,... | collective-permute-start | bytes 8257544 | tf_op jit(solution)/shard_map/ppermute | solution.py:580
  1024.7 68.0 %collective-permute-start = (bf16[3,64,1024]{2,1,0:T(8,128)(2,1)}, bf16[3,64,1024]{2,1,0:T(8,128)(2,1)S(1)}, u32[]{:S(2)}, u32[]{:S(2)}) collective-permute-start(bf16[3,64,1024]{2,1,0:T(8,128)(2,1)} %get-tuple-element.17.small_ref), channel_id=1, source_target_pairs={{1,0},{2,3},{5,4},{6,7},{9,8},{10,11},{13,12},{14,15},{17,16},{18,... | collective-permute-start | bytes 1179656 | tf_op jit(solution)/shard_map/ppermute | solution.py:580
  1026.0 23.5 %copy-start = (bf16[3,448,1024]{2,1,0:T(8,128)(2,1)S(1)}, bf16[3,448,1024]{2,1,0:T(8,128)(2,1)}, u32[]{:S(2)}) copy-start(bf16[3,448,1024]{2,1,0:T(8,128)(2,1)} %get-tuple-element.18.big_ref) | copy-start | bytes 8257540
  1026.0 23.5 %copy-start.1 = (bf16[3,64,1024]{2,1,0:T(8,128)(2,1)S(1)}, bf16[3,64,1024]{2,1,0:T(8,128)(2,1)}, u32[]{:S(2)}) copy-start(bf16[3,64,1024]{2,1,0:T(8,128)(2,1)} %get-tuple-element.17.small_ref) | copy-start | bytes 1179652
  1026.1 23.5 %copy-start.2 = (bf16[8,4,8,512]{3,2,1,0:T(8,128)(2,1)S(1)}, bf16[8,4,8,512]{3,2,1,0:T(8,128)(2,1)}, u32[]{:S(2)}) copy-start(bf16[8,4,8,512]{3,2,1,0:T(8,128)(2,1)} %get-tuple-element.22.refs_2_) | copy-start | bytes 786436
  1026.1 23.5 %copy-start.3 = (f32[8,1024]{1,0:T(8,128)S(1)}, f32[8,1024]{1,0:T(8,128)}, u32[]{:S(2)}) copy-start(f32[8,1024]{1,0:T(8,128)} %get-tuple-element.20.refs_0_) | copy-start | bytes 98308
  1026.1 23.5 %copy-start.4 = (f32[8,1024]{1,0:T(8,128)S(1)}, f32[8,1024]{1,0:T(8,128)}, u32[]{:S(2)}) copy-start(f32[8,1024]{1,0:T(8,128)} %get-tuple-element.21.refs_1_) | copy-start | bytes 98308

commit v4 on v3

--- a/solution.py
+++ b/solution.py
@@ -10,8 +10,8 @@
 MESH = pl.DeviceIdType.MESH
 SLOTS = 4
 ROWS = 16
-HEAD_PARTS = 4
-EDGE = 128
+HEAD_PARTS = 2
+EDGE = 256
 
 
 def kernel(
@@ -33,8 +33,11 @@
     edge_rows = rows - top * EDGE // cols
     bundles = tuple(zip((big_ref, small_ref), splits))
 
+    eager = lax.rem(me, 2) == 1
+    edge_in = outer & eager
+
     def outward(step):
-        return z == 1 if step < 0 else z == ns - 2
+        return (z == 1 if step < 0 else z == ns - 2) & eager
 
     def load_part(part, sem):
         pltpu.make_async_copy(wg_ref.at[0, :, part], fresh.at[0, :, part], sem).start()
@@ -297,13 +300,14 @@
     collect(first_sums, 0)
     divide(0, 0, 0, first_sums, 0, 0, ahead, 4 * ROWS)
     tell(first_sums, 0)
-    both_ways(send_lead)
+    pl.when(eager)(lambda: both_ways(send_lead))
     if experts > 1:
         loaded(1, 0)
         mix(2, 1, 2, tail, 0)
         refill(1, 0)
     collect(head, 1)
     divide(0, 0, 0, head, 0, ahead, cols)
+    pl.when(jnp.logical_not(eager))(lambda: both_ways(send_lead))
     both_ways(send_follow)
     tell(head, 1)
     local_copy(0, 0).start()
@@ -347,7 +351,8 @@
     @pl.when(outer)
     def _():
         local_copy(experts - 1, 1).start()
-        divide_edge()
+
+    pl.when(edge_in)(divide_edge)
 
     for which, ref in enumerate((sg_ref, su_ref)):
         pltpu.make_async_copy(scale.at[which], ref, own_sem.at[1]).start()
@@ -356,7 +361,7 @@
     own_table.start()
     lax.fori_loop(1, ne, send_table, 0)
 
-    @pl.when(outer)
+    @pl.when(edge_in)
     def _():
         spot = place(0, 0, near).at[pl.ds(0, top), pl.ds(0, EDGE)]
         pltpu.make_async_copy(edge16, spot, edge_sem.at[3]).start()
@@ -375,8 +380,8 @@
         for fits, j in ((z >= d, z - d), (z + d < ns, z + d)):
             if isinstance(e, int) and e == 0 and d == 1:
                 short = og_ref.at[0, pl.ds(0, (count - 1) * rows + edge_rows), :]
-                pl.when(fits & outer)(lambda: wait_for(short, recv_sem.at[j, 0]))
-                fits = fits & inner
+                pl.when(fits & edge_in)(lambda: wait_for(short, recv_sem.at[j, 0]))
+                fits = fits & jnp.logical_not(edge_in)
             pl.when(fits)(lambda: wait_for(pieces(count), recv_sem.at[j, e]))
 
     def goes_on(step, d):
@@ -412,7 +417,7 @@
     for d in range(ns - 1):
         for step in (-1, 1):
             pl.when(last_goes(step, d))(lambda: wait_for(pieces(1), last_sent(step, d)))
-    @pl.when(outer)
+    @pl.when(edge_in)
     def _():
         wait_for(edge16, edge_sem.at[3])
 

time: 1090 us -> 1090 us (level)
  no operation moved by 1% of the time
where the time goes in v4:
time: 1090 us
  Pallas kernels  1070 us (98%)
  waiting for transfers between devices  13.1 us (1%)
    pallas_call x1, Pallas kernels, per_device(): pl.pallas_call(functools.partial(kernel, ns, ne, experts, rows, cols, ahe...  1030 us
    pallas_call x1, Pallas kernels, move(): pl.pallas_call(move_kernel, grid=(raw.shape[0],), out_shape=jax.ShapeDtyp...  23.5 us
    pallas_call x1, Pallas kernels, move_all(): pl.pallas_call(functools.partial(move_all_kernel, ns, rows, splits), grid...  22.6 us
  transfers between devices with their start and end apart: 2, of which 2 were waited for; matrix products, arithmetic and copies ran while one was open for 0% of the time, Pallas kernels for 4%

profile of v4, /device:TPU:0, one launch (start us, length us, event | category | flops | bytes accessed | tf_op | source)
XLA Modules:
  0.0 1090.8 jit_solution(1001525230864044543)
XLA Ops:
  0.6 1026.0 %shard_map.110 = (bf16[8,2048,1024]{2,1,0:T(8,128)(2,1)}, bf16[8,2048,1024]{2,1,0:T(8,128)(2,1)}, f32[8,1024]{1,0:T(8,128)}, f32[8,1024]{1,0:T(8,128)}, bf16[3,4...) custom-call(f32[8]{0:T(128)} %mix_ref.1, f32[8,512,1024]{2,1,0:T(8,128)} %wg_ref.1, ...), custom_call_target="tpu_custom_call" | custom-call | tf_op jit(solution)/shard_map/pallas_call | solution.py:548
  1026.6 1.3 collective-permute-start.1
  1027.9 1.3 collective-permute-start
  1029.2 0.0 copy-start
  1029.2 0.0 copy-start.1
  1029.3 0.0 copy-start.2
  1029.3 0.0 copy-start.3
  1029.3 0.0 copy-start.4
  1029.3 23.5 %shard_map.111 = bf16[8,2048,1024]{2,1,0:T(8,128)(2,1)} custom-call(bf16[8,2048,1024]{2,1,0:T(8,128)(2,1)} %get-tuple-element.16.src_ref), custom_call_target="tpu_custom_call" | custom-call | bytes 67108864 | tf_op jit(solution)/shard_map/pallas_call | solution.py:451
  1052.8 0.0 copy-done
  1052.8 0.0 copy-done.1
  1052.8 0.0 copy-done.2
  1052.8 0.0 copy-done.3
  1052.8 0.0 copy-done.4
  1052.8 22.6 %shard_map.112 = (bf16[8,2048,1024]{2,1,0:T(8,128)(2,1)}, f32[8,1024]{1,0:T(8,128)}, f32[8,1024]{1,0:T(8,128)}, bf16[8,4,8,512]{3,2,1,0:T(8,128)(2,1)}) custom-call(bf16[8,2048,1024]{2,1,0:T(8,128)(2,1)} %get-tuple-element.19.raw_ref, bf16[3,448,1024]{2,1,0:T(8,128)(2,1)S(1)} %copy-done, bf16[3,64,1024]{2,1,0:T(8,128)(2,1)S(1)} %copy-done.1, ...), custom_call_target="tpu_custom_call" | custom-call | bytes 67108864 | tf_op jit(solution)/shard_map/pallas_call | solution.py:487
  1075.4 10.4 collective-permute-done.1.pieces_ref
  1085.8 1.6 shard_map.113.whole_ref
  1087.4 2.7 collective-permute-done.pieces_ref
  1090.1 0.8 shard_map.114
Async XLA Ops:
  1026.6 59.2 %collective-permute-start.1 = (bf16[3,448,1024]{2,1,0:T(8,128)(2,1)}, bf16[3,448,1024]{2,1,0:T(8,128)(2,1)S(1)}, u32[]{:S(2)}, u32[]{:S(2)}) collective-permute-start(bf16[3,448,1024]{2,1,0:T(8,128)(2,1)} %get-tuple-element.18.big_ref), channel_id=1, source_target_pairs={{1,0},{2,3},{5,4},{6,7},{9,8},{10,11},{13,12},{14,15},{17,16},{18,... | collective-permute-start | bytes 8257544 | tf_op jit(solution)/shard_map/ppermute | solution.py:585
  1027.9 62.1 %collective-permute-start = (bf16[3,64,1024]{2,1,0:T(8,128)(2,1)}, bf16[3,64,1024]{2,1,0:T(8,128)(2,1)S(1)}, u32[]{:S(2)}, u32[]{:S(2)}) collective-permute-start(bf16[3,64,1024]{2,1,0:T(8,128)(2,1)} %get-tuple-element.17.small_ref), channel_id=1, source_target_pairs={{1,0},{2,3},{5,4},{6,7},{9,8},{10,11},{13,12},{14,15},{17,16},{18,... | collective-permute-start | bytes 1179656 | tf_op jit(solution)/shard_map/ppermute | solution.py:585
  1029.2 23.5 %copy-start = (bf16[3,448,1024]{2,1,0:T(8,128)(2,1)S(1)}, bf16[3,448,1024]{2,1,0:T(8,128)(2,1)}, u32[]{:S(2)}) copy-start(bf16[3,448,1024]{2,1,0:T(8,128)(2,1)} %get-tuple-element.18.big_ref) | copy-start | bytes 8257540
  1029.2 23.5 %copy-start.1 = (bf16[3,64,1024]{2,1,0:T(8,128)(2,1)S(1)}, bf16[3,64,1024]{2,1,0:T(8,128)(2,1)}, u32[]{:S(2)}) copy-start(bf16[3,64,1024]{2,1,0:T(8,128)(2,1)} %get-tuple-element.17.small_ref) | copy-start | bytes 1179652
  1029.3 23.5 %copy-start.2 = (bf16[8,4,8,512]{3,2,1,0:T(8,128)(2,1)S(1)}, bf16[8,4,8,512]{3,2,1,0:T(8,128)(2,1)}, u32[]{:S(2)}) copy-start(bf16[8,4,8,512]{3,2,1,0:T(8,128)(2,1)} %get-tuple-element.22.refs_2_) | copy-start | bytes 786436
  1029.3 23.5 %copy-start.3 = (f32[8,1024]{1,0:T(8,128)S(1)}, f32[8,1024]{1,0:T(8,128)}, u32[]{:S(2)}) copy-start(f32[8,1024]{1,0:T(8,128)} %get-tuple-element.20.refs_0_) | copy-start | bytes 98308
  1029.3 23.5 %copy-start.4 = (f32[8,1024]{1,0:T(8,128)S(1)}, f32[8,1024]{1,0:T(8,128)}, u32[]{:S(2)}) copy-start(f32[8,1024]{1,0:T(8,128)} %get-tuple-element.21.refs_1_) | copy-start | bytes 98308

commit v5 on v4

--- a/solution.py
+++ b/solution.py
@@ -534,7 +534,7 @@
         experts, rows, cols = w_gate.shape
         n = 2 * experts
         ahead = max(cols // HEAD_PARTS // 128, 1) * 128
-        top = rows * 3 // 4 // 16 * 16
+        top = rows // 2 // 16 * 16
         assert top * EDGE % cols == 0
         large = rows * 7 // 8 // 16 * 16
         splits = ((0, large), (large, rows - large))

time: 1090 us -> 1090 us (level)
  no operation moved by 1% of the time
where the time goes in v5:
time: 1090 us
  Pallas kernels  1080 us (99%)
  waiting for transfers between devices  11.9 us (1%)
    pallas_call x1, Pallas kernels, per_device(): pl.pallas_call(functools.partial(kernel, ns, ne, experts, rows, cols, ahe...  1030 us
    pallas_call x1, Pallas kernels, move(): pl.pallas_call(move_kernel, grid=(raw.shape[0],), out_shape=jax.ShapeDtyp...  23.5 us
    pallas_call x1, Pallas kernels, move_all(): pl.pallas_call(functools.partial(move_all_kernel, ns, rows, splits), grid...  22.6 us
  transfers between devices with their start and end apart: 2, of which 2 were waited for; matrix products, arithmetic and copies ran while one was open for 0% of the time, Pallas kernels for 4%

profile of v5, /device:TPU:0, one launch (start us, length us, event | category | flops | bytes accessed | tf_op | source)
XLA Modules:
  0.0 1090.3 jit_solution(5473455937119603831)
XLA Ops:
  0.6 1026.6 %shard_map.110 = (bf16[8,2048,1024]{2,1,0:T(8,128)(2,1)}, bf16[8,2048,1024]{2,1,0:T(8,128)(2,1)}, f32[8,1024]{1,0:T(8,128)}, f32[8,1024]{1,0:T(8,128)}, bf16[3,4...) custom-call(f32[8]{0:T(128)} %mix_ref.1, f32[8,512,1024]{2,1,0:T(8,128)} %wg_ref.1, ...), custom_call_target="tpu_custom_call" | custom-call | tf_op jit(solution)/shard_map/pallas_call | solution.py:548
  1027.3 1.3 collective-permute-start.1
  1028.6 1.3 collective-permute-start
  1029.9 0.0 copy-start
  1029.9 0.0 copy-start.1
  1029.9 0.0 copy-start.2
  1029.9 0.0 copy-start.3
  1029.9 0.0 copy-start.4
  1029.9 23.5 %shard_map.111 = bf16[8,2048,1024]{2,1,0:T(8,128)(2,1)} custom-call(bf16[8,2048,1024]{2,1,0:T(8,128)(2,1)} %get-tuple-element.16.src_ref), custom_call_target="tpu_custom_call" | custom-call | bytes 67108864 | tf_op jit(solution)/shard_map/pallas_call | solution.py:451
  1053.4 0.0 copy-done
  1053.4 0.0 copy-done.1
  1053.4 0.0 copy-done.2
  1053.4 0.0 copy-done.3
  1053.4 0.0 copy-done.4
  1053.4 22.6 %shard_map.112 = (bf16[8,2048,1024]{2,1,0:T(8,128)(2,1)}, f32[8,1024]{1,0:T(8,128)}, f32[8,1024]{1,0:T(8,128)}, bf16[8,4,8,512]{3,2,1,0:T(8,128)(2,1)}) custom-call(bf16[8,2048,1024]{2,1,0:T(8,128)(2,1)} %get-tuple-element.19.raw_ref, bf16[3,448,1024]{2,1,0:T(8,128)(2,1)S(1)} %copy-done, bf16[3,64,1024]{2,1,0:T(8,128)(2,1)S(1)} %copy-done.1, ...), custom_call_target="tpu_custom_call" | custom-call | bytes 67108864 | tf_op jit(solution)/shard_map/pallas_call | solution.py:487
  1076.0 9.2 collective-permute-done.1.pieces_ref
  1085.3 1.6 shard_map.113.whole_ref
  1086.8 2.7 collective-permute-done.pieces_ref
  1089.5 0.8 shard_map.114
Async XLA Ops:
  1027.3 58.0 %collective-permute-start.1 = (bf16[3,448,1024]{2,1,0:T(8,128)(2,1)}, bf16[3,448,1024]{2,1,0:T(8,128)(2,1)S(1)}, u32[]{:S(2)}, u32[]{:S(2)}) collective-permute-start(bf16[3,448,1024]{2,1,0:T(8,128)(2,1)} %get-tuple-element.18.big_ref), channel_id=1, source_target_pairs={{1,0},{2,3},{5,4},{6,7},{9,8},{10,11},{13,12},{14,15},{17,16},{18,... | collective-permute-start | bytes 8257544 | tf_op jit(solution)/shard_map/ppermute | solution.py:585
  1028.6 60.9 %collective-permute-start = (bf16[3,64,1024]{2,1,0:T(8,128)(2,1)}, bf16[3,64,1024]{2,1,0:T(8,128)(2,1)S(1)}, u32[]{:S(2)}, u32[]{:S(2)}) collective-permute-start(bf16[3,64,1024]{2,1,0:T(8,128)(2,1)} %get-tuple-element.17.small_ref), channel_id=1, source_target_pairs={{1,0},{2,3},{5,4},{6,7},{9,8},{10,11},{13,12},{14,15},{17,16},{18,... | collective-permute-start | bytes 1179656 | tf_op jit(solution)/shard_map/ppermute | solution.py:585
  1029.9 23.5 %copy-start = (bf16[3,448,1024]{2,1,0:T(8,128)(2,1)S(1)}, bf16[3,448,1024]{2,1,0:T(8,128)(2,1)}, u32[]{:S(2)}) copy-start(bf16[3,448,1024]{2,1,0:T(8,128)(2,1)} %get-tuple-element.18.big_ref) | copy-start | bytes 8257540
  1029.9 23.5 %copy-start.1 = (bf16[3,64,1024]{2,1,0:T(8,128)(2,1)S(1)}, bf16[3,64,1024]{2,1,0:T(8,128)(2,1)}, u32[]{:S(2)}) copy-start(bf16[3,64,1024]{2,1,0:T(8,128)(2,1)} %get-tuple-element.17.small_ref) | copy-start | bytes 1179652
  1029.9 23.5 %copy-start.2 = (bf16[8,4,8,512]{3,2,1,0:T(8,128)(2,1)S(1)}, bf16[8,4,8,512]{3,2,1,0:T(8,128)(2,1)}, u32[]{:S(2)}) copy-start(bf16[8,4,8,512]{3,2,1,0:T(8,128)(2,1)} %get-tuple-element.22.refs_2_) | copy-start | bytes 786436
  1029.9 23.5 %copy-start.3 = (f32[8,1024]{1,0:T(8,128)S(1)}, f32[8,1024]{1,0:T(8,128)}, u32[]{:S(2)}) copy-start(f32[8,1024]{1,0:T(8,128)} %get-tuple-element.20.refs_0_) | copy-start | bytes 98308
  1029.9 23.5 %copy-start.4 = (f32[8,1024]{1,0:T(8,128)S(1)}, f32[8,1024]{1,0:T(8,128)}, u32[]{:S(2)}) copy-start(f32[8,1024]{1,0:T(8,128)} %get-tuple-element.21.refs_1_) | copy-start | bytes 98308
